TPU v7x, 512 devices: a whole 4x8x8 slice. The times are simulated.
512 devices in a mesh: dm: 16 (over z, core), tm: 32 (over x, y).
Axes of the slice: x: 4, y: 8, z: 8, core: 2. Of those that a mesh axis runs over, the one named last changes fastest.
Arguments:
- dispersed: float32 [4096, 32768], P('dm', 'tm')
- widths: int32 [4], replicated, may hold values from 1 to 129, as said below
Outputs:
- snr: bfloat16 [4, 4096, 32768], P(None, 'dm', 'tm')
- peaks: float32 [4, 4096], P(None, 'dm')
Inputs may be any that keep to these rules, and one draw needn't show every extreme that they name: `widths`: at least one width equals 129.
All inputs are finite; a program needn't handle non-finite values.
Results may differ from a plain program's by a relative error of at most 0.001.
Values sent between devices are 32-bit elements; how exact they have to be, the bound alone decides.
A program may use at most 64 MiB of HBM per device.

v0:
```python
import jax
import jax.numpy as jnp
from jax import lax
from jax.sharding import PartitionSpec as P

HALF = 128


eps_value = 1e-06


def with_halo(x, sides, width):
    for axis, dim in sides:
        peers, length = (lax.axis_size(axis), x.shape[dim])
        up = [(i, (i + 1) % peers) for i in range(peers - 1)]
        down = [(j, i) for i, j in up]
        last = lax.slice_in_dim(x, length - width, length, axis=dim)
        leading = lax.slice_in_dim(x, 0, width, axis=dim)
        before = lax.ppermute(last, axis, up)
        after = lax.ppermute(leading, axis, down)
        x = jnp.concatenate([before, x, after], axis=dim)
    return x


def sent_to_all(x, axis):
    peers = lax.axis_size(axis)
    return lax.all_to_all(jnp.broadcast_to(x[None], (peers, *x.shape)), axis, 0, 0, tiled=True)


def of_everyone(x, axis):
    return sent_to_all(x, axis).sum(axis=0)


def from_behind(block, axis, distance):
    devices = range(lax.axis_size(axis))
    route = [(i - distance, i) for i in devices if i - distance in devices]
    return lax.ppermute(block, axis, route)


def over_copies(x, axis):
    return sent_to_all(x, axis).max(axis=0)


def band_table(span_list, block_len):
    column_idx = jnp.arange(span_list.shape[0] * block_len, dtype=jnp.int32)
    offsets = column_idx % block_len
    reaches = jnp.repeat(span_list, block_len)
    row_idx = jnp.arange(2 * block_len, dtype=jnp.int32)[:, None]
    inside = (row_idx >= offsets[None, :]) & (row_idx < offsets[None, :] + reaches[None, :])
    return inside.astype(jnp.float32)


def window_sum(extended, length, band_matrix, block_len):
    row_count = extended.shape[0]
    block_count = length // block_len
    blocks = extended.reshape(row_count, block_count + 1, block_len)
    paired = jnp.concatenate([blocks[:, :-1], blocks[:, 1:]], axis=2)
    return jnp.einsum("rbs,sk->rbk", paired, band_matrix, precision=lax.Precision.HIGHEST)


def boxcar(extended, length, band_matrix, inverse, block_len):
    row_count = extended.shape[0]
    moving = window_sum(extended, length, band_matrix, block_len)
    moving = moving.reshape(row_count, length // block_len, inverse.shape[0], block_len)
    moving = jnp.transpose(moving, (2, 0, 1, 3)).reshape(inverse.shape[0], row_count, length)
    return moving * inverse[:, None, None]


def body(dispersed, widths):
    row_count, length = dispersed.shape
    block_len = 2 * HALF
    total_len = length * lax.axis_size("tm")
    offset = lax.axis_index("tm") * length
    ma_band = band_table(jnp.full((1,), 2 * HALF + 1, jnp.int32), block_len)
    box_band = band_table(widths, block_len)
    inverse = 1.0 / jnp.sqrt(widths.astype(jnp.float32))

    def counts_at(first_pos, size_len):
        positions = first_pos + jnp.arange(size_len, dtype=jnp.int32)
        counts = (
            jnp.minimum(positions + HALF, total_len - 1) - jnp.maximum(positions - HALF, 0) + 1
        ).astype(jnp.float32)
        inside = (positions >= 0) & (positions < total_len)
        return (counts, inside)

    local_counts = counts_at(offset, length)[0]
    extended = with_halo(dispersed, (("tm", 1),), 2 * HALF)
    wide_counts, inside = counts_at(offset - HALF, length + block_len)
    first_mean = window_sum(extended, length + block_len, ma_band, block_len).reshape(
        row_count, length + block_len
    )
    widened = jnp.where(inside[None, :], first_mean / wide_counts, 0.0)
    smooth_mean = (
        window_sum(widened, length, ma_band, block_len).reshape(row_count, length) / local_counts
    )
    detrended = dispersed - smooth_mean
    padding = jnp.zeros((row_count, HALF), jnp.float32)
    power_sum = of_everyone(jnp.sum(detrended * detrended, axis=1), "tm")
    row_spread_scale = jnp.sqrt(power_sum / total_len + eps_value)
    normed = detrended / row_spread_scale[:, None]
    colsum = of_everyone(jnp.sum(normed, axis=0), "dm")
    cleaned = normed - (colsum / (row_count * lax.axis_size("dm")))[None, :]
    head_cols = from_behind(cleaned[:, :HALF], "tm", -1)
    series = boxcar(
        jnp.concatenate([cleaned, head_cols, padding], axis=1), length, box_band, inverse, block_len
    )
    peak_values = over_copies(jnp.max(series, axis=2), "tm")
    return (series.astype(jnp.bfloat16), peak_values)


def solution(mesh):
    placed = (P("dm", "tm"), P())
    return jax.shard_map(
        body,
        mesh=mesh,
        in_specs=placed,
        out_specs=(P(None, "dm", "tm"), P(None, "dm")),
        check_vma=False,
    )
```

profile of v0, /device:TPU:1, one launch (start us, length us, event | category | flops | bytes accessed | tf_op | source)
XLA Modules:
  0.0 112.7 jit_solution(2209161605111637991)
XLA Ops:
  0.6 1.6 %copy.45 = f32[256,1024]{0,1:T(8,128)S(1)} copy(f32[256,1024]{1,0:T(8,128)} %param.2) | data formatting | bytes 2097152 | tf_op args[0]
  2.2 4.0 %collective-permute-start = (f32[256,256]{0,1:T(8,128)S(1)}, f32[256,256]{0,1:T(8,128)S(1)}, u32[]{:S(2)}, u32[]{:S(2)}) collective-permute-start(f32[256,256]{0,1:T(8,128)S(1)} %get-tuple-element.10), channel_id=1, source_target_pairs={{0,1},{1,2},{2,3},{3,4},{4,5},{5,6},{6,7},{7,8},{8,9},{9,10},{10,1... | collective-permute-start | bytes 786440 | tf_op jit(solution)/shard_map/ppermute | solution.py:19
  6.3 1.3 %collective-permute-start.1 = (f32[256,256]{0,1:T(8,128)S(1)}, f32[256,256]{0,1:T(8,128)S(1)}, u32[]{:S(2)}, u32[]{:S(2)}) collective-permute-start(f32[256,256]{0,1:T(8,128)S(1)} %get-tuple-element.11), channel_id=1, source_target_pairs={{1,0},{2,1},{3,2},{4,3},{5,4},{6,5},{7,6},{8,7},{9,8},{10,9},{11,1... | collective-permute-start | bytes 786440 | tf_op jit(solution)/shard_map/ppermute | solution.py:20
  7.6 1.9 %collective-permute-done = f32[256,256]{0,1:T(8,128)S(1)} collective-permute-done((f32[256,256]{0,1:T(8,128)S(1)}, f32[256,256]{0,1:T(8,128)S(1)}, u32[]{:S(2)}, u32[]{:S(2)}) %collective-permute-start) | collective-permute-done | bytes 262176 | tf_op jit(solution)/shard_map/ppermute | solution.py:19
  9.6 3.8 %collective-permute-done.1 = f32[256,256]{0,1:T(8,128)S(1)} collective-permute-done((f32[256,256]{0,1:T(8,128)S(1)}, f32[256,256]{0,1:T(8,128)S(1)}, u32[]{:S(2)}, u32[]{:S(2)}) %collective-permute-start.1) | collective-permute-done | bytes 262176 | tf_op jit(solution)/shard_map/ppermute | solution.py:20
  13.5 1.3 %fusion.40 = (f32[256,5,256]{0,2,1:T(8,128)}, f32[256,5,256]{0,2,1:T(8,128)S(1)}) fusion(f32[256,6,256]{0,2,1:T(8,128)S(1)} %bitcast.22), kind=kLoop, calls=%fused_computation.58 | loop fusion | bytes 5242880 | tf_op jit(solution)/shard_map/slice | solution.py:57
  14.8 2.8 %copy.57 = f32[256,5,256]{2,0,1:T(8,128)} copy(f32[256,5,256]{0,2,1:T(8,128)} %get-tuple-element.4) | data formatting | bytes 2621440
  17.6 1.5 %copy.58 = f32[256,5,256]{2,0,1:T(8,128)} copy(f32[256,5,256]{0,2,1:T(8,128)S(1)} %get-tuple-element.5) | data formatting | bytes 2621440
  19.0 3.4 %divide_select_fusion = f32[256,5,256]{0,2,1:T(8,128)S(1)} fusion(f32[256,5,256]{2,0,1:T(8,128)} %copy.58, f32[256,5,256]{2,0,1:T(8,128)} %copy.57, f32[5,256]{1,0:T(8,128)S(1)} %add_convert_fusion, pred[5,256]{1,0:T(8,128)(4,1)S(1)} %fusion.31, s32[256]{0:T(256)S(1)} %get-tuple-element.13, s32[256]{0:T(256)S(1)} %get-tuple-element.12), kind=kOutput, calls=%fused_computation.20 | convolution fusion | flops 2014969856 | bytes 3940608 | tf_op jit(solution)/shard_map/rbs,sk->rbk/dot_general | solution.py:58
  22.6 1.3 %fusion.4 = f32[256,4,256]{0,2,1:T(8,128)S(1)} fusion(f32[256,4,256]{0,2,1:T(8,128)S(1)} %get-tuple-element.9, f32[256,4,256]{0,2,1:T(8,128)S(1)} %get-tuple-element.8, s32[256]{0:T(256)S(1)} %get-tuple-element.13, s32[256]{0:T(256)S(1)} %get-tuple-element.12), kind=kOutput, calls=%fused_computation.6 | convolution fusion | flops 1611530240 | bytes 3147776 | tf_op jit(solution)/shard_map/rbs,sk->rbk/dot_general | solution.py:58
  23.9 0.3 multiply_reduce_fusion.1
  24.2 0.6 broadcast_in_dim.27
  24.8 11.5 %all-to-all-start = ((f32[32,1,256]{2,1,0:T(1,128)}), f32[32,1,256]{2,1,0:T(1,128)S(1)}, u32[]{:S(2)}, u32[]{:S(2)}) async-start(f32[32,1,256]{2,1,0:T(1,128)} %broadcast_in_dim.27), calls=%async_computation | async-start | bytes 65536 | tf_op jit(solution)/shard_map/all_to_all | solution.py:27
  36.5 8.7 %all-to-all-done = f32[32,1,256]{2,1,0:T(1,128)S(1)} async-done(((f32[32,1,256]{2,1,0:T(1,128)}), f32[32,1,256]{2,1,0:T(1,128)S(1)}, u32[]{:S(2)}, u32[]{:S(2)}) %all-to-all-start) | async-done | bytes 32800 | tf_op jit(solution)/shard_map/all_to_all | solution.py:27
  45.2 0.2 fusion.22
  45.5 0.7 broadcast_in_dim.28
  46.1 13.6 %all-to-all-start.1 = ((f32[16,1,1024]{2,1,0:T(1,128)}), f32[16,1,1024]{2,1,0:T(1,128)S(1)}, u32[]{:S(2)}, u32[]{:S(2)}) async-start(f32[16,1,1024]{2,1,0:T(1,128)} %broadcast_in_dim.28), calls=%async_computation.1 | async-start | bytes 131072 | tf_op jit(solution)/shard_map/all_to_all | solution.py:27
  59.7 7.8 %all-to-all-done.1 = f32[16,1,1024]{2,1,0:T(1,128)S(1)} async-done(((f32[16,1,1024]{2,1,0:T(1,128)}), f32[16,1,1024]{2,1,0:T(1,128)S(1)}, u32[]{:S(2)}, u32[]{:S(2)}) %all-to-all-start.1) | async-done | bytes 65568 | tf_op jit(solution)/shard_map/all_to_all | solution.py:27
  67.8 1.3 %collective-permute-start.2 = (f32[256,128]{0,1:T(8,128)S(1)}, f32[256,128]{0,1:T(8,128)S(1)}, u32[]{:S(2)}, u32[]{:S(2)}) collective-permute-start(f32[256,128]{0,1:T(8,128)S(1)} %slice.42), channel_id=1, source_target_pairs={{1,0},{2,1},{3,2},{4,3},{5,4},{6,5},{7,6},{8,7},{9,8},{10,9},{11,1... | collective-permute-start | bytes 393224 | tf_op jit(solution)/shard_map/ppermute | solution.py:37
  69.1 5.5 %collective-permute-done.2 = f32[256,128]{0,1:T(8,128)S(1)} collective-permute-done((f32[256,128]{0,1:T(8,128)S(1)}, f32[256,128]{0,1:T(8,128)S(1)}, u32[]{:S(2)}, u32[]{:S(2)}) %collective-permute-start.2) | collective-permute-done | bytes 131104 | tf_op jit(solution)/shard_map/ppermute | solution.py:37
  74.6 0.2 maximum_maximum_fusion
  75.0 0.3 copy.59
  75.3 0.3 copy.60
  75.7 5.2 %fusion.8 = f32[256,4,1024]{2,0,1:T(8,128)} fusion(f32[256,4,256]{2,0,1:T(8,128)S(1)} %copy.60, f32[256,4,256]{2,0,1:T(8,128)S(1)} %copy.59, s32[1024]{0:T(1024)S(1)} %get-tuple-element.15, s32[1024]{0:T(1024)S(1)} %get-tuple-element.14), kind=kOutput, calls=%fused_computation.10 | convolution fusion | flops 6444548096 | bytes 6299648 | tf_op jit(solution)/shard_map/rbs,sk->rbk/dot_general | solution.py:58
  80.9 5.6 %reshape.114 = f32[256,4,4,256]{3,2,0,1:T(4,128)} reshape(f32[256,4,1024]{2,0,1:T(8,128)} %fusion.8) | data formatting | bytes 8388608 | tf_op jit(solution)/shard_map/reshape | solution.py:64
  86.5 3.2 %multiply_reduce_fusion = f32[4,256]{0,1:T(8,128)S(1)} fusion(f32[4]{0:T(128)S(1)} %convert_rsqrt_fusion, f32[256,4,4,256]{3,2,0,1:T(4,128)} %reshape.114), kind=kLoop, calls=%fused_computation | loop fusion | flops 2096128 | bytes 4198416 | tf_op jit(solution)/shard_map/reduce_max | solution.py:107
  89.8 0.7 broadcast_in_dim.31
  90.5 4.8 %all-to-all-start.2 = ((f32[32,4,256]{2,1,0:T(4,128)}), f32[32,4,256]{2,1,0:T(4,128)S(1)}, u32[]{:S(2)}, u32[]{:S(2)}) async-start(f32[32,4,256]{2,1,0:T(4,128)} %broadcast_in_dim.31), calls=%async_computation.2 | async-start | bytes 262144 | tf_op jit(solution)/shard_map/all_to_all | solution.py:27
  95.3 6.9 %copy.50 = f32[4,256,4,256]{3,2,1,0:T(4,128)} copy(f32[4,256,4,256]{3,0,1,2:T(4,128)} %bitcast.21) | data formatting | bytes 8388608 | tf_op jit(solution)/shard_map/transpose | solution.py:65
  102.2 5.8 %reshape.115 = f32[4,256,1024]{2,1,0:T(8,128)} reshape(f32[4,256,4,256]{3,2,1,0:T(4,128)} %copy.50) | data formatting | bytes 8388608 | tf_op jit(solution)/shard_map/reshape | solution.py:65
  107.9 4.1 %multiply_convert_fusion = bf16[4,256,1024]{2,1,0:T(8,128)(2,1)} fusion(f32[4,256,1024]{2,1,0:T(8,128)} %reshape.115, f32[4]{0:T(128)S(1)} %convert_rsqrt_fusion), kind=kLoop, calls=%fused_computation.1 | loop fusion | flops 2097152 | bytes 6291472 | tf_op jit(solution)/shard_map/convert_element_type | solution.py:108
  112.1 0.6 reduce_max.19
  (24 shorter events, 1.0 us)
Async XLA Ops:
  2.2 7.3 %collective-permute-start = (f32[256,256]{0,1:T(8,128)S(1)}, f32[256,256]{0,1:T(8,128)S(1)}, u32[]{:S(2)}, u32[]{:S(2)}) collective-permute-start(f32[256,256]{0,1:T(8,128)S(1)} %get-tuple-element.10), channel_id=1, source_target_pairs={{0,1},{1,2},{2,3},{3,4},{4,5},{5,6},{6,7},{7,8},{8,9},{9,10},{10,1... | collective-permute-start | bytes 786440 | tf_op jit(solution)/shard_map/ppermute | solution.py:19
  6.3 7.1 %collective-permute-start.1 = (f32[256,256]{0,1:T(8,128)S(1)}, f32[256,256]{0,1:T(8,128)S(1)}, u32[]{:S(2)}, u32[]{:S(2)}) collective-permute-start(f32[256,256]{0,1:T(8,128)S(1)} %get-tuple-element.11), channel_id=1, source_target_pairs={{1,0},{2,1},{3,2},{4,3},{5,4},{6,5},{7,6},{8,7},{9,8},{10,9},{11,1... | collective-permute-start | bytes 786440 | tf_op jit(solution)/shard_map/ppermute | solution.py:20
  23.9 12.5 %copy-start = (s32[4]{0:T(128)S(1)}, s32[4]{0:T(128)}, u32[]{:S(2)}) copy-start(s32[4]{0:T(128)} %param.3) | copy-start | bytes 52
  24.8 20.3 %all-to-all-start = ((f32[32,1,256]{2,1,0:T(1,128)}), f32[32,1,256]{2,1,0:T(1,128)S(1)}, u32[]{:S(2)}, u32[]{:S(2)}) async-start(f32[32,1,256]{2,1,0:T(1,128)} %broadcast_in_dim.27), calls=%async_computation | async-start | bytes 65536 | tf_op jit(solution)/shard_map/all_to_all | solution.py:27
  46.1 21.3 %all-to-all-start.1 = ((f32[16,1,1024]{2,1,0:T(1,128)}), f32[16,1,1024]{2,1,0:T(1,128)S(1)}, u32[]{:S(2)}, u32[]{:S(2)}) async-start(f32[16,1,1024]{2,1,0:T(1,128)} %broadcast_in_dim.28), calls=%async_computation.1 | async-start | bytes 131072 | tf_op jit(solution)/shard_map/all_to_all | solution.py:27
  67.8 6.8 %collective-permute-start.2 = (f32[256,128]{0,1:T(8,128)S(1)}, f32[256,128]{0,1:T(8,128)S(1)}, u32[]{:S(2)}, u32[]{:S(2)}) collective-permute-start(f32[256,128]{0,1:T(8,128)S(1)} %slice.42), channel_id=1, source_target_pairs={{1,0},{2,1},{3,2},{4,3},{5,4},{6,5},{7,6},{8,7},{9,8},{10,9},{11,1... | collective-permute-start | bytes 393224 | tf_op jit(solution)/shard_map/ppermute | solution.py:37
  90.5 21.6 %all-to-all-start.2 = ((f32[32,4,256]{2,1,0:T(4,128)}), f32[32,4,256]{2,1,0:T(4,128)S(1)}, u32[]{:S(2)}, u32[]{:S(2)}) async-start(f32[32,4,256]{2,1,0:T(4,128)} %broadcast_in_dim.31), calls=%async_computation.2 | async-start | bytes 262144 | tf_op jit(solution)/shard_map/all_to_all | solution.py:27
where the time goes:
time: 113 us
  starting transfers between devices  36.6 us (32%)
  local copies, waits for them, and re-layouts  28.6 us (25%)
  waiting for transfers between devices  27.7 us (25%)
  matrix products  9.89 us (9%)
  other arithmetic  9.15 us (8%)
    all_to_all x3, starting transfers between devices, sent_to_all(): lax.all_to_all(jnp.broadcast_to(x[None], (peers, *x.shape)), axis, 0, 0,...  30 us
    all_to_all x3, waiting for transfers between devices, sent_to_all(): lax.all_to_all(jnp.broadcast_to(x[None], (peers, *x.shape)), axis, 0, 0,...  16.4 us
    dot_general x3, matrix products, window_sum(): jnp.einsum('rbs,sk->rbk', paired, band_matrix, precision=lax.Precision.HI...  9.89 us
    transpose x1, local copies, waits for them, and re-layouts, boxcar(): jnp.transpose(moving, (2, 0, 1, 3))  6.86 us
    unnamed x9, local copies, waits for them, and re-layouts  6.54 us
    reshape x1, local copies, waits for them, and re-layouts, boxcar(): jnp.transpose(moving, (2, 0, 1, 3))  5.78 us
    reshape x1, local copies, waits for them, and re-layouts, boxcar(): moving.reshape(row_count, length // block_len, inverse.shape[0], block_len)  5.62 us
    ppermute x1, waiting for transfers between devices, from_behind(): return lax.ppermute(block, axis, route)  5.52 us
  transfers between devices with their start and end apart: 6, of which 5 were waited for; matrix products, arithmetic and copies ran while one was open for 15% of the time, Pallas kernels for 0%

commit v1 on v0

v1 whole, which is shorter than its diff:
```python
import functools

import jax
import jax.numpy as jnp
from jax import lax
from jax.experimental import pallas as pl
from jax.experimental.pallas import tpu as pltpu
from jax.sharding import PartitionSpec as P

MESH = pl.DeviceIdType.MESH
HALF = 128
BLOCK = 2 * HALF
EPS = 1e-06
CHUNKS = 4


def parts_of(x):
    high = x.astype(jnp.bfloat16)
    rest = x - high.astype(jnp.float32)
    mid = rest.astype(jnp.bfloat16)
    low = (rest - mid.astype(jnp.float32)).astype(jnp.bfloat16)
    return high, mid, low


def banded(x, band):
    return jnp.dot(jnp.concatenate(parts_of(x), axis=1), band, preferred_element_type=jnp.float32)


def peer_offsets(peers):
    side = 8 if peers % 8 == 0 else peers
    other = peers // side
    steps = [(dx, dy) for dx in range(other) for dy in range(side) if dx or dy]
    reach = lambda s: min(s[0], other - s[0]) + min(s[1], side - s[1])
    return side, other, sorted(steps, key=reach, reverse=True)


def kernel(
    tm_size, dm_size, widths, x, snr, peaks,
    ext, low_band, high_band, box_band, fm, part, det, split, boxed, out, rows_max,
    power_out, power_in, scale, col_out, col_in, common, box_common, peak_out, peak_in,
    load_sem, halo_send, halo_recv, head_send, head_recv,
    power_send, power_recv, col_send, col_recv, peak_send, peak_recv, store_sem,
):
    rows, length = x.shape
    boxes = widths.shape[0]
    blocks = length // BLOCK
    tiles = length // HALF
    total_len = length * tm_size
    tm = lax.axis_index("tm")
    dm = lax.axis_index("dm")
    right, left = lax.rem(tm + 1, tm_size), lax.rem(tm + tm_size - 1, tm_size)
    side, other, steps = peer_offsets(tm_size)
    tm_x, tm_y = tm // side, tm % side

    def tm_peer(step):
        return lax.rem(tm_x + step[0], other) * side + lax.rem(tm_y + step[1], side)

    dm_steps = sorted(range(1, dm_size), key=lambda d: min(d, dm_size - d), reverse=True)

    barrier = pltpu.get_barrier_semaphore()
    for step in steps:
        pl.semaphore_signal(barrier, inc=1, device_id={"tm": tm_peer(step)}, device_id_type=MESH)
    for d in dm_steps:
        pl.semaphore_signal(
            barrier, inc=1, device_id={"dm": lax.rem(dm + d, dm_size)}, device_id_type=MESH
        )
    loads = {}
    for b in [1, blocks] + list(range(2, blocks)):
        loads[b] = pltpu.make_async_copy(
            x.at[:, pl.ds((b - 1) * BLOCK, BLOCK)], ext.at[b], load_sem.at[b - 1]
        )
        loads[b].start()

    row_idx = lax.broadcasted_iota(jnp.int32, (BLOCK, BLOCK), 0)
    col_idx = lax.broadcasted_iota(jnp.int32, (BLOCK, BLOCK), 1)
    low = (row_idx >= col_idx).astype(jnp.float32).astype(jnp.bfloat16)
    high = (row_idx <= col_idx).astype(jnp.float32).astype(jnp.bfloat16)
    lane = lax.broadcasted_iota(jnp.int32, (BLOCK, HALF), 1)
    depth = lax.broadcasted_iota(jnp.int32, (BLOCK, HALF), 0)
    for k in range(3):
        low_band[pl.ds(k * BLOCK, BLOCK), :] = low
        high_band[pl.ds(k * BLOCK, BLOCK), :] = high
    for i in range(boxes):
        inside = (depth >= lane) & (depth < lane + widths[i])
        for k in range(3):
            box_band[pl.ds(k * BLOCK, BLOCK), pl.ds(i * HALF, HALF)] = inside.astype(
                jnp.float32
            ).astype(jnp.bfloat16)

    def inverse_counts(first):
        pos = first + lax.broadcasted_iota(jnp.int32, (1, BLOCK), 1)
        counts = (jnp.minimum(pos + HALF, total_len - 1) - jnp.maximum(pos - HALF, 0) + 1)
        valid = (pos >= 0) & (pos < total_len)
        return jnp.where(valid, 1.0 / jnp.maximum(counts, 1).astype(jnp.float32), 0.0)

    offset = tm * length
    inner = 1.0 / (2 * HALF + 1)
    edge_first = inverse_counts(offset - HALF)
    edge_last = inverse_counts(offset + length - HALF)
    own_first = inverse_counts(offset)
    own_last = inverse_counts(offset + length - BLOCK)

    loads[1].wait()
    loads[blocks].wait()
    pl.semaphore_wait(barrier, len(steps) + len(dm_steps))
    chunk = rows // CHUNKS
    halos = []
    for q in range(CHUNKS):
        span = pl.ds(q * chunk, chunk)
        to_right = pltpu.make_async_remote_copy(
            src_ref=ext.at[blocks, span], dst_ref=ext.at[0, span],
            send_sem=halo_send.at[0, q], recv_sem=halo_recv.at[0, q],
            device_id={"tm": right}, device_id_type=MESH,
        )
        to_left = pltpu.make_async_remote_copy(
            src_ref=ext.at[1, span], dst_ref=ext.at[blocks + 1, span],
            send_sem=halo_send.at[1, q], recv_sem=halo_recv.at[1, q],
            device_id={"tm": left}, device_id_type=MESH,
        )
        to_right.start()
        to_left.start()
        halos.append((to_right, to_left))

    for b in range(2, blocks):
        loads[b].wait()
    part[0] = banded(ext[1], high_band[...])
    part[1] = banded(ext[blocks], low_band[...])
    for b in range(1, blocks):
        sums = banded(ext[b], low_band[...]) + banded(ext[b + 1], high_band[...])
        fm[b] = sums * inner
    part[2] = banded(fm[1], high_band[...])
    part[3] = banded(fm[blocks - 1], low_band[...])

    def keep(block_idx, span, values):
        for k, piece in enumerate(parts_of(values)):
            split[k, span, pl.ds(block_idx * BLOCK, BLOCK)] = piece
        det[span, pl.ds(block_idx * BLOCK, BLOCK)] = values
        squares = values * values
        return squares[:, :HALF] + squares[:, HALF:]

    power = jnp.zeros((rows, HALF), jnp.float32)
    for b in range(1, blocks - 1):
        smooth = (banded(fm[b], low_band[...]) + banded(fm[b + 1], high_band[...])) * inner
        power = power + keep(b, pl.ds(0, rows), ext[b + 1] - smooth)
    rows_max[0] = power

    def box_sums(t):
        window = jnp.concatenate(
            [split[k, :, pl.ds(t * HALF, BLOCK)] for k in range(3)], axis=1
        )
        boxed[t] = jnp.dot(window, box_band[...], preferred_element_type=jnp.float32)

    early = range(BLOCK // HALF, tiles - 3)
    for t in early:
        box_sums(t)

    is_first = tm == 0
    is_last = tm == tm_size - 1
    for q in range(CHUNKS):
        span = pl.ds(q * chunk, chunk)
        halos[q][0].wait_recv()
        before = jnp.where(is_first, 0.0, ext[0, span])
        mean = (part[0, span] + banded(before, low_band[...])) * edge_first
        smooth = (part[2, span] + banded(mean, low_band[...])) * own_first
        power = keep(0, span, ext[1, span] - smooth)
        halos[q][1].wait_recv()
        after = jnp.where(is_last, 0.0, ext[blocks + 1, span])
        mean = (part[1, span] + banded(after, high_band[...])) * edge_last
        smooth = (part[3, span] + banded(mean, high_band[...])) * own_last
        power = power + keep(blocks - 1, span, ext[blocks, span] - smooth)
        rows_max[0, span] = rows_max[0, span] + power

    for h in range(rows // HALF):
        turned = rows_max[0, pl.ds(h * HALF, HALF)].T
        power_out[pl.ds(h, 1), :] = jnp.sum(turned, axis=0, keepdims=True)

    def to_peers(src, dst, send_sem, recv_sem):
        for step in steps:
            pltpu.make_async_remote_copy(
                src_ref=src, dst_ref=dst.at[step[0] * side + step[1] - 1],
                send_sem=send_sem, recv_sem=recv_sem,
                device_id={"tm": tm_peer(step)}, device_id_type=MESH,
            ).start()

    to_peers(power_out, power_in, power_send, power_recv)
    head = pltpu.make_async_remote_copy(
        src_ref=det.at[:, pl.ds(0, HALF)], dst_ref=det.at[:, pl.ds(length, HALF)],
        send_sem=head_send, recv_sem=head_recv,
        device_id={"tm": left}, device_id_type=MESH,
    )
    head.start()

    for t in range(tiles - 1):
        if t not in early:
            box_sums(t)
    pltpu.make_async_copy(power_in, power_in, power_recv).wait()
    totals = power_out[...] + jnp.sum(power_in[...], axis=0)
    inverse_scale = 1.0 / jnp.sqrt(totals * (1.0 / total_len) + EPS)
    for h in range(rows // HALF):
        row = jnp.broadcast_to(inverse_scale[h:h + 1, :], (HALF, HALF))
        scale[pl.ds(h * HALF, HALF), :] = row.T

    head.wait_recv()
    head_values = jnp.where(is_last, 0.0, det[:, pl.ds(length, HALF)])

    def column_sum(values):
        weighted = (values * scale[...]).reshape(rows // 8, 8, HALF)
        return jnp.sum(jnp.sum(weighted, axis=0), axis=0, keepdims=True)

    for t in range(tiles):
        col_out[pl.ds(t, 1), :] = column_sum(det[:, pl.ds(t * HALF, HALF)])
    col_out[pl.ds(tiles, 1), :] = column_sum(head_values)
    for d in dm_steps:
        pltpu.make_async_remote_copy(
            src_ref=col_out, dst_ref=col_in.at[d - 1], send_sem=col_send, recv_sem=col_recv,
            device_id={"dm": lax.rem(dm + d, dm_size)}, device_id_type=MESH,
        ).start()

    for k, piece in enumerate(parts_of(head_values)):
        split[k, :, pl.ds(length, HALF)] = piece
    box_sums(tiles - 1)

    inverse = []
    for i in range(boxes):
        width = jnp.full((16, HALF), widths[i], jnp.int32).astype(jnp.float32)
        inverse.append(1.0 / jnp.sqrt(width))

    pltpu.make_async_copy(col_in, col_in, col_recv).wait()
    column_total = col_out[...] + jnp.sum(col_in[...], axis=0)
    common[...] = column_total * (1.0 / (rows * dm_size))
    window = jnp.concatenate([common[pl.ds(0, tiles), :], common[pl.ds(1, tiles), :]], axis=1)
    box_common[...] = banded(window, box_band[...])

    stores = []
    for i in range(boxes):
        offsets = [
            jnp.broadcast_to(box_common[pl.ds(t, 1), pl.ds(i * HALF, HALF)], (16, HALF)) * inverse[i]
            for t in range(tiles)
        ]

        def some_rows(r, carry):
            span = pl.ds(pl.multiple_of(r * 16, 16), 16)
            gain = scale[span, :] * inverse[i]
            most = None
            for t in range(tiles):
                series = boxed[t, span, pl.ds(i * HALF, HALF)] * gain - offsets[t]
                most = series if most is None else jnp.maximum(most, series)
                out[i, span, pl.ds(t * HALF, HALF)] = series.astype(jnp.bfloat16)
            rows_max[i, span] = most
            return carry

        lax.fori_loop(0, rows // 16, some_rows, 0)
        stores.append(pltpu.make_async_copy(out.at[i], snr.at[i], store_sem.at[i]))
        stores[-1].start()

    halves = rows // HALF
    for i in range(boxes):
        for h in range(halves):
            turned = rows_max[i, pl.ds(h * HALF, HALF)].T
            peak_out[pl.ds(i * halves + h, 1), :] = jnp.max(turned, axis=0, keepdims=True)
    to_peers(peak_out, peak_in, peak_send, peak_recv)
    pltpu.make_async_copy(peak_in, peak_in, peak_recv).wait()
    most = jnp.maximum(peak_out[...], jnp.max(peak_in[...], axis=0))
    for i in range(boxes):
        for h in range(halves):
            row = i * halves + h
            peaks[pl.ds(i, 1), pl.ds(h * HALF, HALF)] = most[row:row + 1, :]

    for to_right, to_left in halos:
        to_right.wait_send()
        to_left.wait_send()
    head.wait_send()
    pltpu.make_async_copy(power_in, power_in, power_send).wait()
    pltpu.make_async_copy(col_in, col_in, col_send).wait()
    pltpu.make_async_copy(peak_in, peak_in, peak_send).wait()
    for store in stores:
        store.wait()


def solution(mesh):
    tm_size, dm_size = mesh.shape["tm"], mesh.shape["dm"]

    def step(dispersed, widths):
        rows, length = dispersed.shape
        boxes = widths.shape[0]
        blocks, tiles, halves = length // BLOCK, length // HALF, rows // HALF
        f32, bf16 = jnp.float32, jnp.bfloat16
        dma = pltpu.SemaphoreType.DMA
        return pl.pallas_call(
            functools.partial(kernel, tm_size, dm_size),
            out_shape=(
                jax.ShapeDtypeStruct((boxes, rows, length), bf16),
                jax.ShapeDtypeStruct((boxes, rows), f32),
            ),
            in_specs=[
                pl.BlockSpec(memory_space=pltpu.SMEM),
                pl.BlockSpec(memory_space=pl.ANY),
            ],
            out_specs=(
                pl.BlockSpec(memory_space=pl.ANY),
                pl.BlockSpec(memory_space=pltpu.VMEM),
            ),
            scratch_shapes=[
                pltpu.VMEM((blocks + 2, rows, BLOCK), f32),
                pltpu.VMEM((3 * BLOCK, BLOCK), bf16),
                pltpu.VMEM((3 * BLOCK, BLOCK), bf16),
                pltpu.VMEM((3 * BLOCK, boxes * HALF), bf16),
                pltpu.VMEM((blocks, rows, BLOCK), f32),
                pltpu.VMEM((4, rows, BLOCK), f32),
                pltpu.VMEM((rows, length + HALF), f32),
                pltpu.VMEM((3, rows, length + HALF), bf16),
                pltpu.VMEM((tiles, rows, boxes * HALF), f32),
                pltpu.VMEM((boxes, rows, length), bf16),
                pltpu.VMEM((boxes, rows, HALF), f32),
                pltpu.VMEM((halves, HALF), f32),
                pltpu.VMEM((tm_size - 1, halves, HALF), f32),
                pltpu.VMEM((rows, HALF), f32),
                pltpu.VMEM((tiles + 1, HALF), f32),
                pltpu.VMEM((dm_size - 1, tiles + 1, HALF), f32),
                pltpu.VMEM((tiles + 1, HALF), f32),
                pltpu.VMEM((tiles, boxes * HALF), f32),
                pltpu.VMEM((boxes * halves, HALF), f32),
                pltpu.VMEM((tm_size - 1, boxes * halves, HALF), f32),
                dma((blocks,)),
                dma((2, CHUNKS)),
                dma((2, CHUNKS)),
                dma, dma, dma, dma, dma, dma, dma, dma,
                dma((boxes,)),
            ],
            compiler_params=pltpu.CompilerParams(
                collective_id=0, has_side_effects=True, vmem_limit_bytes=48 * 2**20
            ),
        )(widths, dispersed)

    return jax.shard_map(
        step,
        mesh=mesh,
        in_specs=(P("dm", "tm"), P()),
        out_specs=(P(None, "dm", "tm"), P(None, "dm")),
        check_vma=False,
    )
```

time: 113 us -> 48.4 us (0.43)
  Pallas kernels: 0 us -> 43.8 us
  starting transfers between devices: 36.6 us -> 0 us
  waiting for transfers between devices: 27.7 us -> 0 us
  local copies, waits for them, and re-layouts: 28.6 us -> 3.79 us
  matrix products: 9.89 us -> 0 us
  other arithmetic: 9.15 us -> 0 us
    pallas_call x0 -> x1, Pallas kernels: none -> 43.8 us  [step(): pl.pallas_call(functools.partial(kernel, tm_size, dm_size), out_shape=(ja...]
    all_to_all x3 -> x0, starting transfers between devices: 30 us -> none  [sent_to_all(): lax.all_to_all(jnp.broadcast_to(x[None], (peers, *x.shape)), axis, 0, 0,...]
    all_to_all x3 -> x0, waiting for transfers between devices: 16.4 us -> none  [sent_to_all(): lax.all_to_all(jnp.broadcast_to(x[None], (peers, *x.shape)), axis, 0, 0,...]
    reshape x2 -> x0, local copies, waits for them, and re-layouts: 11.4 us -> none  [the longest x1 5.78 us: boxcar(): jnp.transpose(moving, (2, 0, 1, 3))]
    ppermute x3 -> x0, waiting for transfers between devices: 11.3 us -> none  [the longest x1 5.52 us: from_behind(): return lax.ppermute(block, axis, route)]
    dot_general x3 -> x0, matrix products: 9.89 us -> none  [window_sum(): jnp.einsum('rbs,sk->rbk', paired, band_matrix, precision=lax.Precision.HI...]
    transpose x1 -> x0, local copies, waits for them, and re-layouts: 6.86 us -> none  [boxcar(): jnp.transpose(moving, (2, 0, 1, 3))]
    ppermute x3 -> x0, starting transfers between devices: 6.62 us -> none  [the longest x1 4.03 us: with_halo(): before = lax.ppermute(last, axis, up)]
  transfers between devices with their start and end apart: 6 -> 0, of which waited for: 5 -> 0; matrix products, arithmetic and copies ran while one was open for 15% -> 0% of each run, Pallas kernels for 0% -> 0%
where the time goes in v1:
time: 48.4 us; the launch traced here: 48.3 us
  Pallas kernels  43.8 us (90%)
  local copies, waits for them, and re-layouts  3.79 us (8%)
  between operations  0.65 us (1%)
    pallas_call x1, Pallas kernels, step(): pl.pallas_call(functools.partial(kernel, tm_size, dm_size), out_shape=(ja...  43.8 us
    unnamed x6, local copies, waits for them, and re-layouts  3.79 us

profile of v1, /device:TPU:1, one launch (start us, length us, event | category | flops | bytes accessed | tf_op | source)
XLA Modules:
  0.0 48.3 jit_solution(5658900566455015164)
XLA Ops:
  0.6 0.0 copy-start
  0.6 1.2 %copy-done = f32[256,1024]{1,0:T(8,128)S(1)} copy-done((f32[256,1024]{1,0:T(8,128)S(1)}, f32[256,1024]{1,0:T(8,128)}, u32[]{:S(2)}) %copy-start) | copy-done | bytes 1048600
  1.9 0.0 copy-start.1
  1.9 0.7 %copy-done.1 = s32[4]{0:T(128)S(1)} copy-done((s32[4]{0:T(128)S(1)}, s32[4]{0:T(128)}, u32[]{:S(2)}) %copy-start.1) | copy-done | bytes 40
  2.5 43.8 %shard_map.41 = (bf16[4,256,1024]{2,1,0:T(8,128)(2,1)S(1)}, f32[4,256]{1,0:T(4,128)S(1)}) custom-call(s32[4]{0:T(128)S(1)} %copy-done.1, f32[256,1024]{1,0:T(8,128)S(1)} %copy-done), custom_call_target="tpu_custom_call" | custom-call | tf_op jit(solution)/shard_map/pallas_call | solution.py:289
  46.3 1.3 %copy.6 = bf16[4,256,1024]{2,1,0:T(8,128)(2,1)} copy(bf16[4,256,1024]{2,1,0:T(8,128)(2,1)S(1)} %get-tuple-element.4) | data formatting | bytes 4194304
  47.7 0.6 %copy.7 = f32[4,256]{1,0:T(4,128)} copy(f32[4,256]{1,0:T(4,128)S(1)} %get-tuple-element.5) | data formatting | bytes 8192
Async XLA Ops:
  0.6 1.2 %copy-start = (f32[256,1024]{1,0:T(8,128)S(1)}, f32[256,1024]{1,0:T(8,128)}, u32[]{:S(2)}) copy-start(f32[256,1024]{1,0:T(8,128)} %x.1) | copy-start | bytes 3145732
  1.9 0.7 %copy-start.1 = (s32[4]{0:T(128)S(1)}, s32[4]{0:T(128)}, u32[]{:S(2)}) copy-start(s32[4]{0:T(128)} %widths.1) | copy-start | bytes 52

commit v2 on v1

--- a/solution.py
+++ b/solution.py
@@ -23,7 +23,10 @@
 
 
 def banded(x, band):
-    return jnp.dot(jnp.concatenate(parts_of(x), axis=1), band, preferred_element_type=jnp.float32)
+    rows = x.shape[0]
+    stacked = jnp.concatenate(parts_of(x), axis=0)
+    sums = jnp.dot(stacked, band, preferred_element_type=jnp.float32)
+    return sums[:rows] + sums[rows:2 * rows] + sums[2 * rows:]
 
 
 def peer_offsets(peers):
@@ -35,11 +38,11 @@
 
 
 def kernel(
-    tm_size, dm_size, widths, x, snr, peaks,
-    ext, low_band, high_band, box_band, fm, part, det, split, boxed, out, rows_max,
+    tm_size, dm_size, widths_in, x, snr, peaks,
+    widths, widths_sem, ext, low_band, high_band, box_band, fm, part, det, split, boxed, rows_max,
     power_out, power_in, scale, col_out, col_in, common, box_common, peak_out, peak_in,
     load_sem, halo_send, halo_recv, head_send, head_recv,
-    power_send, power_recv, col_send, col_recv, peak_send, peak_recv, store_sem,
+    power_send, power_recv, col_send, col_recv, peak_send, peak_recv, dm_known, tm_tokens, dm_tokens,
 ):
     rows, length = x.shape
     boxes = widths.shape[0]
@@ -58,12 +61,18 @@
     dm_steps = sorted(range(1, dm_size), key=lambda d: min(d, dm_size - d), reverse=True)
 
     barrier = pltpu.get_barrier_semaphore()
-    for step in steps:
-        pl.semaphore_signal(barrier, inc=1, device_id={"tm": tm_peer(step)}, device_id_type=MESH)
-    for d in dm_steps:
+    near = sorted({1, tm_size - 1})
+    for d in near:
         pl.semaphore_signal(
-            barrier, inc=1, device_id={"dm": lax.rem(dm + d, dm_size)}, device_id_type=MESH
+            barrier, inc=1, device_id={"tm": lax.rem(tm + d, tm_size)}, device_id_type=MESH
         )
+
+    @pl.when(dm < dm_size - 1)
+    def _():
+        pl.semaphore_signal(barrier, inc=1, device_id={"dm": dm + 1}, device_id_type=MESH)
+
+    fetch = pltpu.make_async_copy(widths_in, widths, widths_sem)
+    fetch.start()
     loads = {}
     for b in [1, blocks] + list(range(2, blocks)):
         loads[b] = pltpu.make_async_copy(
@@ -71,15 +80,52 @@
         )
         loads[b].start()
 
+    tm_rounds = [d for d in (1, 2, 4, 8, 16, 32) if 2 * d < tm_size]
+    dm_rounds = [d for d in (1, 2, 4, 8, 16, 32) if d < dm_size - 1]
+
+    def tm_tell(n):
+        if n < len(tm_rounds):
+            for d in {tm_rounds[n], tm_size - tm_rounds[n]}:
+                pl.semaphore_signal(
+                    tm_tokens.at[n], inc=1, device_id={"tm": lax.rem(tm + d, tm_size)},
+                    device_id_type=MESH,
+                )
+
+    def tm_hear(n):
+        if n < len(tm_rounds):
+            pl.semaphore_wait(tm_tokens.at[n], len({tm_rounds[n], tm_size - tm_rounds[n]}))
+
+    def dm_tell(n):
+        if n < len(dm_rounds):
+            d = dm_rounds[n]
+
+            @pl.when(dm + d < dm_size)
+            def _():
+                pl.semaphore_signal(
+                    dm_tokens.at[n], inc=1, device_id={"dm": dm + d}, device_id_type=MESH
+                )
+
+            @pl.when(dm >= d)
+            def _():
+                pl.semaphore_signal(
+                    dm_tokens.at[n], inc=1, device_id={"dm": dm - d}, device_id_type=MESH
+                )
+
+    def dm_hear(n):
+        if n < len(dm_rounds):
+            d = dm_rounds[n]
+            ahead = jnp.minimum((dm_size - 1 - dm) // d, 1)
+            pl.semaphore_wait(dm_tokens.at[n], ahead + jnp.minimum(dm // d, 1))
+
     row_idx = lax.broadcasted_iota(jnp.int32, (BLOCK, BLOCK), 0)
     col_idx = lax.broadcasted_iota(jnp.int32, (BLOCK, BLOCK), 1)
     low = (row_idx >= col_idx).astype(jnp.float32).astype(jnp.bfloat16)
     high = (row_idx <= col_idx).astype(jnp.float32).astype(jnp.bfloat16)
     lane = lax.broadcasted_iota(jnp.int32, (BLOCK, HALF), 1)
     depth = lax.broadcasted_iota(jnp.int32, (BLOCK, HALF), 0)
-    for k in range(3):
-        low_band[pl.ds(k * BLOCK, BLOCK), :] = low
-        high_band[pl.ds(k * BLOCK, BLOCK), :] = high
+    low_band[...] = low
+    high_band[...] = high
+    fetch.wait()
     for i in range(boxes):
         inside = (depth >= lane) & (depth < lane + widths[i])
         for k in range(3):
@@ -102,7 +148,7 @@
 
     loads[1].wait()
     loads[blocks].wait()
-    pl.semaphore_wait(barrier, len(steps) + len(dm_steps))
+    pl.semaphore_wait(barrier, len(near) + jnp.minimum(dm, 1))
     chunk = rows // CHUNKS
     halos = []
     for q in range(CHUNKS):
@@ -121,6 +167,12 @@
         to_left.start()
         halos.append((to_right, to_left))
 
+    @pl.when(dm > 0)
+    def _():
+        pl.semaphore_signal(dm_known, inc=1, device_id={"dm": dm - 1}, device_id_type=MESH)
+
+    tm_tell(0)
+
     for b in range(2, blocks):
         loads[b].wait()
     part[0] = banded(ext[1], high_band[...])
@@ -128,6 +180,15 @@
     for b in range(1, blocks):
         sums = banded(ext[b], low_band[...]) + banded(ext[b + 1], high_band[...])
         fm[b] = sums * inner
+        if b == 1:
+            tm_hear(0)
+            tm_tell(1)
+
+    @pl.when(dm < dm_size - 1)
+    def _():
+        pl.semaphore_wait(dm_known, 1)
+
+    dm_tell(0)
     part[2] = banded(fm[1], high_band[...])
     part[3] = banded(fm[blocks - 1], low_band[...])
 
@@ -143,6 +204,8 @@
         smooth = (banded(fm[b], low_band[...]) + banded(fm[b + 1], high_band[...])) * inner
         power = power + keep(b, pl.ds(0, rows), ext[b + 1] - smooth)
     rows_max[0] = power
+    tm_hear(1)
+    tm_tell(2)
 
     def box_sums(t):
         window = jnp.concatenate(
@@ -159,20 +222,27 @@
     for q in range(CHUNKS):
         span = pl.ds(q * chunk, chunk)
         halos[q][0].wait_recv()
+        halos[q][1].wait_recv()
         before = jnp.where(is_first, 0.0, ext[0, span])
         mean = (part[0, span] + banded(before, low_band[...])) * edge_first
         smooth = (part[2, span] + banded(mean, low_band[...])) * own_first
+        after = jnp.where(is_last, 0.0, ext[blocks + 1, span])
+        mean_after = (part[1, span] + banded(after, high_band[...])) * edge_last
+        smooth_after = (part[3, span] + banded(mean_after, high_band[...])) * own_last
         power = keep(0, span, ext[1, span] - smooth)
-        halos[q][1].wait_recv()
-        after = jnp.where(is_last, 0.0, ext[blocks + 1, span])
-        mean = (part[1, span] + banded(after, high_band[...])) * edge_last
-        smooth = (part[3, span] + banded(mean, high_band[...])) * own_last
-        power = power + keep(blocks - 1, span, ext[blocks, span] - smooth)
+        power = power + keep(blocks - 1, span, ext[blocks, span] - smooth_after)
         rows_max[0, span] = rows_max[0, span] + power
+        if q == 1:
+            tm_hear(2)
+            tm_tell(3)
 
     for h in range(rows // HALF):
         turned = rows_max[0, pl.ds(h * HALF, HALF)].T
         power_out[pl.ds(h, 1), :] = jnp.sum(turned, axis=0, keepdims=True)
+
+    for n in range(3, len(tm_rounds)):
+        tm_hear(n)
+        tm_tell(n + 1)
 
     def to_peers(src, dst, send_sem, recv_sem):
         for step in steps:
@@ -193,6 +263,9 @@
     for t in range(tiles - 1):
         if t not in early:
             box_sums(t)
+    for n in range(len(dm_rounds)):
+        dm_hear(n)
+        dm_tell(n + 1)
     pltpu.make_async_copy(power_in, power_in, power_recv).wait()
     totals = power_out[...] + jnp.sum(power_in[...], axis=0)
     inverse_scale = 1.0 / jnp.sqrt(totals * (1.0 / total_len) + EPS)
@@ -229,9 +302,8 @@
     column_total = col_out[...] + jnp.sum(col_in[...], axis=0)
     common[...] = column_total * (1.0 / (rows * dm_size))
     window = jnp.concatenate([common[pl.ds(0, tiles), :], common[pl.ds(1, tiles), :]], axis=1)
-    box_common[...] = banded(window, box_band[...])
-
-    stores = []
+    box_common[...] = banded(window, box_band[pl.ds(0, BLOCK), :])
+
     for i in range(boxes):
         offsets = [
             jnp.broadcast_to(box_common[pl.ds(t, 1), pl.ds(i * HALF, HALF)], (16, HALF)) * inverse[i]
@@ -245,13 +317,11 @@
             for t in range(tiles):
                 series = boxed[t, span, pl.ds(i * HALF, HALF)] * gain - offsets[t]
                 most = series if most is None else jnp.maximum(most, series)
-                out[i, span, pl.ds(t * HALF, HALF)] = series.astype(jnp.bfloat16)
+                snr[i, span, pl.ds(t * HALF, HALF)] = series.astype(jnp.bfloat16)
             rows_max[i, span] = most
             return carry
 
         lax.fori_loop(0, rows // 16, some_rows, 0)
-        stores.append(pltpu.make_async_copy(out.at[i], snr.at[i], store_sem.at[i]))
-        stores[-1].start()
 
     halves = rows // HALF
     for i in range(boxes):
@@ -273,8 +343,16 @@
     pltpu.make_async_copy(power_in, power_in, power_send).wait()
     pltpu.make_async_copy(col_in, col_in, col_send).wait()
     pltpu.make_async_copy(peak_in, peak_in, peak_send).wait()
-    for store in stores:
-        store.wait()
+
+
+def hand_out(snr, peaks, snr_out, peaks_out, sems):
+    boxes = snr.shape[0]
+    copies = [pltpu.make_async_copy(peaks, peaks_out, sems.at[boxes])]
+    copies += [pltpu.make_async_copy(snr.at[i], snr_out.at[i], sems.at[i]) for i in range(boxes)]
+    for copy in copies:
+        copy.start()
+    for copy in copies:
+        copy.wait()
 
 
 def solution(mesh):
@@ -286,31 +364,27 @@
         blocks, tiles, halves = length // BLOCK, length // HALF, rows // HALF
         f32, bf16 = jnp.float32, jnp.bfloat16
         dma = pltpu.SemaphoreType.DMA
-        return pl.pallas_call(
+        inputs = [pltpu.with_memory_space_constraint(a, pltpu.HBM) for a in (widths, dispersed)]
+        snr, peaks = pl.pallas_call(
             functools.partial(kernel, tm_size, dm_size),
             out_shape=(
-                jax.ShapeDtypeStruct((boxes, rows, length), bf16),
-                jax.ShapeDtypeStruct((boxes, rows), f32),
+                pltpu.VMEM((boxes, rows, length), bf16),
+                pltpu.VMEM((boxes, rows), f32),
             ),
-            in_specs=[
-                pl.BlockSpec(memory_space=pltpu.SMEM),
-                pl.BlockSpec(memory_space=pl.ANY),
-            ],
-            out_specs=(
-                pl.BlockSpec(memory_space=pl.ANY),
-                pl.BlockSpec(memory_space=pltpu.VMEM),
-            ),
+            in_specs=[pl.BlockSpec(memory_space=pltpu.HBM)] * 2,
+            out_specs=(pl.BlockSpec(memory_space=pltpu.VMEM),) * 2,
             scratch_shapes=[
+                pltpu.SMEM((boxes,), jnp.int32),
+                dma,
                 pltpu.VMEM((blocks + 2, rows, BLOCK), f32),
-                pltpu.VMEM((3 * BLOCK, BLOCK), bf16),
-                pltpu.VMEM((3 * BLOCK, BLOCK), bf16),
+                pltpu.VMEM((BLOCK, BLOCK), bf16),
+                pltpu.VMEM((BLOCK, BLOCK), bf16),
                 pltpu.VMEM((3 * BLOCK, boxes * HALF), bf16),
                 pltpu.VMEM((blocks, rows, BLOCK), f32),
                 pltpu.VMEM((4, rows, BLOCK), f32),
                 pltpu.VMEM((rows, length + HALF), f32),
                 pltpu.VMEM((3, rows, length + HALF), bf16),
                 pltpu.VMEM((tiles, rows, boxes * HALF), f32),
-                pltpu.VMEM((boxes, rows, length), bf16),
                 pltpu.VMEM((boxes, rows, HALF), f32),
                 pltpu.VMEM((halves, HALF), f32),
                 pltpu.VMEM((tm_size - 1, halves, HALF), f32),
@@ -325,12 +399,25 @@
                 dma((2, CHUNKS)),
                 dma((2, CHUNKS)),
                 dma, dma, dma, dma, dma, dma, dma, dma,
-                dma((boxes,)),
+                pltpu.SemaphoreType.REGULAR,
+                pltpu.SemaphoreType.REGULAR((5,)),
+                pltpu.SemaphoreType.REGULAR((5,)),
             ],
             compiler_params=pltpu.CompilerParams(
                 collective_id=0, has_side_effects=True, vmem_limit_bytes=48 * 2**20
             ),
-        )(widths, dispersed)
+        )(*inputs)
+        return pl.pallas_call(
+            hand_out,
+            out_shape=(
+                jax.ShapeDtypeStruct(snr.shape, bf16),
+                jax.ShapeDtypeStruct(peaks.shape, f32),
+            ),
+            in_specs=[pl.BlockSpec(memory_space=pl.ANY)] * 2,
+            out_specs=(pl.BlockSpec(memory_space=pl.ANY),) * 2,
+            scratch_shapes=[dma((boxes + 1,))],
+            compiler_params=pltpu.CompilerParams(vmem_limit_bytes=2**22),
+        )(snr, peaks)
 
     return jax.shard_map(
         step,

time: 48.4 us -> 45.2 us (0.934)
  local copies, waits for them, and re-layouts: 3.79 us -> 0 us
  Pallas kernels: 43.8 us -> 44.4 us
    unnamed x6 -> x0, local copies, waits for them, and re-layouts: 3.79 us -> none
    pallas_call x1 -> x2, Pallas kernels: 43.8 us -> 44.4 us  [the longest x1 43.1 us: step(): pl.pallas_call(functools.partial(kernel, tm_size, dm_size), out_shape=(pl...]
where the time goes in v2:
time: 45.2 us; the launch traced here: 45.1 us
  Pallas kernels  44.4 us (98%)
  between operations  0.64 us (1%)
    pallas_call x1, Pallas kernels, step(): pl.pallas_call(functools.partial(kernel, tm_size, dm_size), out_shape=(pl...  43.1 us
    pallas_call x1, Pallas kernels, step(): pl.pallas_call(hand_out, out_shape=(jax.ShapeDtypeStruct(snr.shape, bf16)...  1.36 us

profile of v2, /device:TPU:1, one launch (start us, length us, event | category | flops | bytes accessed | tf_op | source)
XLA Modules:
  0.0 45.1 jit_solution(5830866598468980147)
XLA Ops:
  0.6 43.1 %shard_map.41 = (bf16[4,256,1024]{2,1,0:T(8,128)(2,1)S(1)}, f32[4,256]{1,0:T(4,128)S(1)}) custom-call(s32[4]{0:T(128)} %widths_in.1, f32[256,1024]{1,0:T(8,128)} %x.1), custom_call_target="tpu_custom_call" | custom-call | tf_op jit(solution)/shard_map/pallas_call | solution.py:368
  43.7 1.4 %shard_map.42 = (bf16[4,256,1024]{2,1,0:T(8,128)(2,1)}, f32[4,256]{1,0:T(4,128)}) custom-call(bf16[4,256,1024]{2,1,0:T(8,128)(2,1)S(1)} %get-tuple-element.4.snr, f32[4,256]{1,0:T(4,128)S(1)} %get-tuple-element.5.peaks), custom_call_target="tpu_custom_call" | custom-call | tf_op jit(solution)/shard_map/pallas_call | solution.py:410

commit v3 on v2

v3 whole, which is shorter than its diff:
```python
import functools

import jax
import jax.numpy as jnp
from jax import lax
from jax.experimental import pallas as pl
from jax.experimental.pallas import tpu as pltpu
from jax.sharding import PartitionSpec as P

MESH = pl.DeviceIdType.MESH
HALF = 128
BLOCK = 2 * HALF
EPS = 1e-06
CHUNKS = (80, 80, 64, 32)


def parts_of(x):
    high = x.astype(jnp.bfloat16)
    rest = x - high.astype(jnp.float32)
    mid = rest.astype(jnp.bfloat16)
    low = (rest - mid.astype(jnp.float32)).astype(jnp.bfloat16)
    return high, mid, low


def banded(x, band):
    rows = x.shape[0]
    stacked = jnp.concatenate(parts_of(x), axis=0)
    sums = jnp.dot(stacked, band, preferred_element_type=jnp.float32)
    return sums[:rows] + sums[rows:2 * rows] + sums[2 * rows:]


def peer_offsets(peers):
    side = 8 if peers % 8 == 0 else peers
    other = peers // side
    steps = [(dx, dy) for dx in range(other) for dy in range(side) if dx or dy]
    reach = lambda s: min(s[0], other - s[0]) + min(s[1], side - s[1])
    return side, other, sorted(steps, key=reach, reverse=True)


def kernel(
    tm_size, dm_size, widths_in, x, snr, peaks,
    widths, widths_sem, ext, low_band, high_band, low_twice, high_twice, box_band, fm, part, det, split, boxed, rows_max,
    power_out, power_in, scale, col_out, col_in, common, box_common, peak_out, peak_in,
    edge_sem, load_sem, halo_send, halo_recv, head_send, head_recv,
    power_send, power_recv, col_send, col_recv, peak_send, peak_recv, tm_known, dm_known,
):
    rows, length = x.shape
    boxes = widths.shape[0]
    blocks = length // BLOCK
    tiles = length // HALF
    total_len = length * tm_size
    tm = lax.axis_index("tm")
    dm = lax.axis_index("dm")
    right, left = lax.rem(tm + 1, tm_size), lax.rem(tm + tm_size - 1, tm_size)
    side, other, steps = peer_offsets(tm_size)
    tm_x, tm_y = tm // side, tm % side

    def tm_peer(step):
        return lax.rem(tm_x + step[0], other) * side + lax.rem(tm_y + step[1], side)

    dm_steps = sorted(range(1, dm_size), key=lambda d: min(d, dm_size - d), reverse=True)

    spans = [pl.ds(sum(CHUNKS[:q]), CHUNKS[q]) for q in range(len(CHUNKS))]
    edge_loads = []
    for q, span in enumerate(spans):
        for b in (blocks, 1):
            edge_loads.append(
                pltpu.make_async_copy(
                    x.at[span, pl.ds((b - 1) * BLOCK, BLOCK)], ext.at[b, span],
                    edge_sem.at[int(b == 1), q],
                )
            )
            edge_loads[-1].start()

    dm_hub = dm_size - 1
    hub_x, hub_y = other // 2, lax.rem(side // 2 + 1, side)
    tm_hub = hub_x * side + hub_y
    is_first, is_last = tm == 0, tm == tm_size - 1
    near_hub = (tm >= tm_hub - 1) & (tm <= tm_hub + 1)
    barrier = pltpu.get_barrier_semaphore()

    def greet(peer):
        pl.semaphore_signal(barrier, inc=1, device_id=peer, device_id_type=MESH)

    @pl.when(jnp.logical_not(is_first))
    def _():
        greet({"tm": left})

    @pl.when(jnp.logical_not(is_last))
    def _():
        greet({"tm": right})

    @pl.when(jnp.logical_not(near_hub))
    def _():
        greet({"tm": tm_hub})

    @pl.when(dm != dm_hub)
    def _():
        greet({"dm": dm_hub})

    beside = jnp.minimum(tm, 1) + jnp.minimum(tm_size - 1 - tm, 1)
    greetings = jnp.where(tm == tm_hub, tm_size - 1, beside)
    greetings = greetings + jnp.where(dm == dm_hub, dm_size - 1, 0)

    for load in edge_loads[:2]:
        load.wait()
    pl.semaphore_wait(barrier, greetings)
    to_right, to_left = [], []
    for q, span in enumerate(spans):
        to_right.append(
            pltpu.make_async_remote_copy(
                src_ref=ext.at[blocks, span], dst_ref=ext.at[0, span],
                send_sem=halo_send.at[0, q], recv_sem=halo_recv.at[0, q],
                device_id={"tm": right}, device_id_type=MESH,
            )
        )
        to_left.append(
            pltpu.make_async_remote_copy(
                src_ref=ext.at[1, span], dst_ref=ext.at[blocks + 1, span],
                send_sem=halo_send.at[1, q], recv_sem=halo_recv.at[1, q],
                device_id={"tm": left}, device_id_type=MESH,
            )
        )
    for q in range(len(spans)):
        if q > 0:
            edge_loads[2 * q].wait()
            edge_loads[2 * q + 1].wait()

        @pl.when(jnp.logical_not(is_last))
        def _():
            to_right[q].start()

        @pl.when(jnp.logical_not(is_first))
        def _():
            to_left[q].start()

    loads = {}
    for b in range(2, blocks):
        loads[b] = pltpu.make_async_copy(
            x.at[:, pl.ds((b - 1) * BLOCK, BLOCK)], ext.at[b], load_sem.at[b - 1]
        )
        loads[b].start()
    fetch = pltpu.make_async_copy(widths_in, widths, widths_sem)
    fetch.start()

    @pl.when(tm == tm_hub)
    def _():
        for step in steps:
            pl.semaphore_signal(
                tm_known, inc=1, device_id={"tm": tm_peer(step)}, device_id_type=MESH
            )

    @pl.when(dm == dm_hub)
    def _():
        for d in range(dm_size - 1):
            pl.semaphore_signal(dm_known, inc=1, device_id={"dm": d}, device_id_type=MESH)

    row_idx = lax.broadcasted_iota(jnp.int32, (BLOCK, BLOCK), 0)
    col_idx = lax.broadcasted_iota(jnp.int32, (BLOCK, BLOCK), 1)
    low = (row_idx >= col_idx).astype(jnp.float32).astype(jnp.bfloat16)
    high = (row_idx <= col_idx).astype(jnp.float32).astype(jnp.bfloat16)
    low_band[...] = low
    high_band[...] = high
    span_len = (row_idx - col_idx).astype(jnp.float32)
    low_twice[...] = jnp.maximum(span_len + 1.0, 0.0).astype(jnp.bfloat16)
    high_twice[...] = jnp.maximum(1.0 - span_len, 0.0).astype(jnp.bfloat16)

    def inverse_counts(first):
        pos = first + lax.broadcasted_iota(jnp.int32, (1, BLOCK), 1)
        counts = (jnp.minimum(pos + HALF, total_len - 1) - jnp.maximum(pos - HALF, 0) + 1)
        valid = (pos >= 0) & (pos < total_len)
        return jnp.where(valid, 1.0 / jnp.maximum(counts, 1).astype(jnp.float32), 0.0)

    offset = tm * length
    inner = 1.0 / (2 * HALF + 1)
    edge_first = inverse_counts(offset - HALF)
    edge_last = inverse_counts(offset + length - HALF)
    own_first = inverse_counts(offset)
    own_last = inverse_counts(offset + length - BLOCK)

    for b in range(2, blocks):
        loads[b].wait()
    for b in range(1, blocks):
        sums = banded(ext[b], low_band[...]) + banded(ext[b + 1], high_band[...])
        fm[b] = sums * inner
    mean = banded(ext[1], high_band[...]) * edge_first
    smooth = banded(fm[1], high_band[...]) + banded(mean, low_band[...])
    part[0] = ext[1] - smooth * own_first
    mean = banded(ext[blocks], low_band[...]) * edge_last
    smooth = banded(fm[blocks - 1], low_band[...]) + banded(mean, high_band[...])
    part[1] = ext[blocks] - smooth * own_last

    def keep(block_idx, span, values):
        for k, piece in enumerate(parts_of(values)):
            split[k, span, pl.ds(block_idx * BLOCK, BLOCK)] = piece
        det[span, pl.ds(block_idx * BLOCK, BLOCK)] = values
        squares = values * values
        return squares[:, :HALF] + squares[:, HALF:]

    power = jnp.zeros((rows, HALF), jnp.float32)
    for b in range(1, blocks - 1):
        smooth = (banded(fm[b], low_band[...]) + banded(fm[b + 1], high_band[...])) * inner
        power = power + keep(b, pl.ds(0, rows), ext[b + 1] - smooth)
    rows_max[0] = power

    for q, span in enumerate(spans):
        @pl.when(jnp.logical_not(is_first))
        def _():
            to_right[q].wait_recv()

        @pl.when(jnp.logical_not(is_last))
        def _():
            to_left[q].wait_recv()

        before = jnp.where(is_first, 0.0, ext[0, span])
        after = jnp.where(is_last, 0.0, ext[blocks + 1, span])
        from_before = banded(before, low_twice[...]) * (inner * inner)
        from_after = banded(after, high_twice[...]) * (inner * inner)
        power = keep(0, span, part[0, span] - from_before)
        power = power + keep(blocks - 1, span, part[1, span] - from_after)
        rows_max[0, span] = rows_max[0, span] + power

    for h in range(rows // HALF):
        turned = rows_max[0, pl.ds(h * HALF, HALF)].T
        power_out[pl.ds(h, 1), :] = jnp.sum(turned, axis=0, keepdims=True)

    @pl.when(tm != tm_hub)
    def _():
        pl.semaphore_wait(tm_known, 1)

    def to_peers(src, dst, send_sem, recv_sem):
        for step in steps:
            pltpu.make_async_remote_copy(
                src_ref=src, dst_ref=dst.at[step[0] * side + step[1] - 1],
                send_sem=send_sem, recv_sem=recv_sem,
                device_id={"tm": tm_peer(step)}, device_id_type=MESH,
            ).start()

    to_peers(power_out, power_in, power_send, power_recv)
    head = pltpu.make_async_remote_copy(
        src_ref=det.at[:, pl.ds(0, HALF)], dst_ref=det.at[:, pl.ds(length, HALF)],
        send_sem=head_send, recv_sem=head_recv,
        device_id={"tm": left}, device_id_type=MESH,
    )

    @pl.when(jnp.logical_not(is_first))
    def _():
        head.start()


    fetch.wait()
    lane = lax.broadcasted_iota(jnp.int32, (BLOCK, HALF), 1)
    depth = lax.broadcasted_iota(jnp.int32, (BLOCK, HALF), 0)
    for i in range(boxes):
        inside = (depth >= lane) & (depth < lane + widths[i])
        for k in range(3):
            box_band[pl.ds(k * BLOCK, BLOCK), pl.ds(i * HALF, HALF)] = inside.astype(
                jnp.float32
            ).astype(jnp.bfloat16)

    def box_sums(t):
        window = jnp.concatenate(
            [split[k, :, pl.ds(t * HALF, BLOCK)] for k in range(3)], axis=1
        )
        boxed[t] = jnp.dot(window, box_band[...], preferred_element_type=jnp.float32)

    for t in range(tiles - 1):
        box_sums(t)

    @pl.when(dm != dm_hub)
    def _():
        pl.semaphore_wait(dm_known, 1)

    pltpu.make_async_copy(power_in, power_in, power_recv).wait()
    totals = power_out[...] + jnp.sum(power_in[...], axis=0)
    inverse_scale = 1.0 / jnp.sqrt(totals * (1.0 / total_len) + EPS)
    for h in range(rows // HALF):
        row = jnp.broadcast_to(inverse_scale[h:h + 1, :], (HALF, HALF))
        scale[pl.ds(h * HALF, HALF), :] = row.T

    @pl.when(jnp.logical_not(is_last))
    def _():
        head.wait_recv()

    det[:, pl.ds(length, HALF)] = jnp.where(is_last, 0.0, det[:, pl.ds(length, HALF)])
    sums = [jnp.zeros((8, HALF), jnp.float32) for _ in range(tiles + 1)]
    for r in range(rows // 8):
        gain = scale[pl.ds(r * 8, 8), :]
        for t in range(tiles + 1):
            sums[t] = sums[t] + det[pl.ds(r * 8, 8), pl.ds(t * HALF, HALF)] * gain
    for t in range(tiles + 1):
        col_out[pl.ds(t, 1), :] = jnp.sum(sums[t], axis=0, keepdims=True)
    for d in dm_steps:
        pltpu.make_async_remote_copy(
            src_ref=col_out, dst_ref=col_in.at[d - 1], send_sem=col_send, recv_sem=col_recv,
            device_id={"dm": lax.rem(dm + d, dm_size)}, device_id_type=MESH,
        ).start()

    for k, piece in enumerate(parts_of(det[:, pl.ds(length, HALF)])):
        split[k, :, pl.ds(length, HALF)] = piece
    box_sums(tiles - 1)

    inverse = []
    for i in range(boxes):
        width = jnp.full((16, HALF), widths[i], jnp.int32).astype(jnp.float32)
        inverse.append(1.0 / jnp.sqrt(width))

    pltpu.make_async_copy(col_in, col_in, col_recv).wait()
    column_total = col_out[...] + jnp.sum(col_in[...], axis=0)
    common[...] = column_total * (1.0 / (rows * dm_size))
    window = jnp.concatenate([common[pl.ds(0, tiles), :], common[pl.ds(1, tiles), :]], axis=1)
    box_common[...] = banded(window, box_band[pl.ds(0, BLOCK), :])

    for i in range(boxes):
        offsets = [
            jnp.broadcast_to(box_common[pl.ds(t, 1), pl.ds(i * HALF, HALF)], (16, HALF)) * inverse[i]
            for t in range(tiles)
        ]

        def some_rows(r, carry):
            for k in range(4):
                span = pl.ds(pl.multiple_of(r * 64 + k * 16, 16), 16)
                gain = scale[span, :] * inverse[i]
                most = None
                for t in range(tiles):
                    series = boxed[t, span, pl.ds(i * HALF, HALF)] * gain - offsets[t]
                    most = series if most is None else jnp.maximum(most, series)
                    snr[i, span, pl.ds(t * HALF, HALF)] = series.astype(jnp.bfloat16)
                rows_max[i, span] = most
            return carry

        lax.fori_loop(0, rows // 64, some_rows, 0)

    halves = rows // HALF
    for i in range(boxes):
        for h in range(halves):
            turned = rows_max[i, pl.ds(h * HALF, HALF)].T
            peak_out[pl.ds(i * halves + h, 1), :] = jnp.max(turned, axis=0, keepdims=True)
    to_peers(peak_out, peak_in, peak_send, peak_recv)
    pltpu.make_async_copy(peak_in, peak_in, peak_recv).wait()
    most = jnp.maximum(peak_out[...], jnp.max(peak_in[...], axis=0))
    for i in range(boxes):
        for h in range(halves):
            row = i * halves + h
            peaks[pl.ds(i, 1), pl.ds(h * HALF, HALF)] = most[row:row + 1, :]

    @pl.when(jnp.logical_not(is_last))
    def _():
        for copy in to_right:
            copy.wait_send()

    @pl.when(jnp.logical_not(is_first))
    def _():
        for copy in to_left:
            copy.wait_send()
        head.wait_send()

    pltpu.make_async_copy(power_in, power_in, power_send).wait()
    pltpu.make_async_copy(col_in, col_in, col_send).wait()
    pltpu.make_async_copy(peak_in, peak_in, peak_send).wait()


def hand_out(snr, peaks, snr_out, peaks_out, sems):
    boxes = snr.shape[0]
    copies = [pltpu.make_async_copy(peaks, peaks_out, sems.at[boxes])]
    copies += [pltpu.make_async_copy(snr.at[i], snr_out.at[i], sems.at[i]) for i in range(boxes)]
    for copy in copies:
        copy.start()
    for copy in copies:
        copy.wait()


def solution(mesh):
    tm_size, dm_size = mesh.shape["tm"], mesh.shape["dm"]

    def step(dispersed, widths):
        rows, length = dispersed.shape
        boxes = widths.shape[0]
        blocks, tiles, halves = length // BLOCK, length // HALF, rows // HALF
        f32, bf16 = jnp.float32, jnp.bfloat16
        dma = pltpu.SemaphoreType.DMA
        inputs = [pltpu.with_memory_space_constraint(a, pltpu.HBM) for a in (widths, dispersed)]
        snr, peaks = pl.pallas_call(
            functools.partial(kernel, tm_size, dm_size),
            out_shape=(
                pltpu.VMEM((boxes, rows, length), bf16),
                pltpu.VMEM((boxes, rows), f32),
            ),
            in_specs=[pl.BlockSpec(memory_space=pltpu.HBM)] * 2,
            out_specs=(pl.BlockSpec(memory_space=pltpu.VMEM),) * 2,
            scratch_shapes=[
                pltpu.SMEM((boxes,), jnp.int32),
                dma,
                pltpu.VMEM((blocks + 2, rows, BLOCK), f32),
                pltpu.VMEM((BLOCK, BLOCK), bf16),
                pltpu.VMEM((BLOCK, BLOCK), bf16),
                pltpu.VMEM((BLOCK, BLOCK), bf16),
                pltpu.VMEM((BLOCK, BLOCK), bf16),
                pltpu.VMEM((3 * BLOCK, boxes * HALF), bf16),
                pltpu.VMEM((blocks, rows, BLOCK), f32),
                pltpu.VMEM((2, rows, BLOCK), f32),
                pltpu.VMEM((rows, length + HALF), f32),
                pltpu.VMEM((3, rows, length + HALF), bf16),
                pltpu.VMEM((tiles, rows, boxes * HALF), f32),
                pltpu.VMEM((boxes, rows, HALF), f32),
                pltpu.VMEM((halves, HALF), f32),
                pltpu.VMEM((tm_size - 1, halves, HALF), f32),
                pltpu.VMEM((rows, HALF), f32),
                pltpu.VMEM((tiles + 1, HALF), f32),
                pltpu.VMEM((dm_size - 1, tiles + 1, HALF), f32),
                pltpu.VMEM((tiles + 1, HALF), f32),
                pltpu.VMEM((tiles, boxes * HALF), f32),
                pltpu.VMEM((boxes * halves, HALF), f32),
                pltpu.VMEM((tm_size - 1, boxes * halves, HALF), f32),
                dma((2, len(CHUNKS))),
                dma((blocks,)),
                dma((2, len(CHUNKS))),
                dma((2, len(CHUNKS))),
                dma, dma, dma, dma, dma, dma, dma, dma,
                pltpu.SemaphoreType.REGULAR,
                pltpu.SemaphoreType.REGULAR,
            ],
            compiler_params=pltpu.CompilerParams(
                collective_id=0, has_side_effects=True, vmem_limit_bytes=48 * 2**20
            ),
        )(*inputs)
        return pl.pallas_call(
            hand_out,
            out_shape=(
                jax.ShapeDtypeStruct(snr.shape, bf16),
                jax.ShapeDtypeStruct(peaks.shape, f32),
            ),
            in_specs=[pl.BlockSpec(memory_space=pl.ANY)] * 2,
            out_specs=(pl.BlockSpec(memory_space=pl.ANY),) * 2,
            scratch_shapes=[dma((boxes + 1,))],
            compiler_params=pltpu.CompilerParams(vmem_limit_bytes=2**22),
        )(snr, peaks)

    return jax.shard_map(
        step,
        mesh=mesh,
        in_specs=(P("dm", "tm"), P()),
        out_specs=(P(None, "dm", "tm"), P(None, "dm")),
        check_vma=False,
    )
```

time: 45.2 us -> 41.6 us (0.920)
  Pallas kernels: 44.4 us -> 40.8 us
    pallas_call x1, Pallas kernels: 43.1 us -> 39.4 us  [step(): pl.pallas_call(functools.partial(kernel, tm_size, dm_size), out_shape=(pl...]
where the time goes in v3:
time: 41.6 us; the launch traced here: 41.4 us
  Pallas kernels  40.8 us (98%)
  between operations  0.64 us (2%)
    pallas_call x1, Pallas kernels, step(): pl.pallas_call(functools.partial(kernel, tm_size, dm_size), out_shape=(pl...  39.4 us
    pallas_call x1, Pallas kernels, step(): pl.pallas_call(hand_out, out_shape=(jax.ShapeDtypeStruct(snr.shape, bf16)...  1.36 us

profile of v3, /device:TPU:1, one launch (start us, length us, event | category | flops | bytes accessed | tf_op | source)
XLA Modules:
  0.0 41.4 jit_solution(2349595441554677012)
XLA Ops:
  0.6 39.4 %shard_map.41 = (bf16[4,256,1024]{2,1,0:T(8,128)(2,1)S(1)}, f32[4,256]{1,0:T(4,128)S(1)}) custom-call(s32[4]{0:T(128)} %widths_in.1, f32[256,1024]{1,0:T(8,128)} %x.1), custom_call_target="tpu_custom_call" | custom-call | tf_op jit(solution)/shard_map/pallas_call | solution.py:383
  40.1 1.4 %shard_map.42 = (bf16[4,256,1024]{2,1,0:T(8,128)(2,1)}, f32[4,256]{1,0:T(4,128)}) custom-call(bf16[4,256,1024]{2,1,0:T(8,128)(2,1)S(1)} %get-tuple-element.4.snr, f32[4,256]{1,0:T(4,128)S(1)} %get-tuple-element.5.peaks), custom_call_target="tpu_custom_call" | custom-call | tf_op jit(solution)/shard_map/pallas_call | solution.py:427

commit v4 on v3

--- a/solution.py
+++ b/solution.py
@@ -29,6 +29,10 @@
     return sums[:rows] + sums[rows:2 * rows] + sums[2 * rows:]
 
 
+def wrapped(index, size):
+    return jnp.where(index >= size, index - size, index)
+
+
 def peer_offsets(peers):
     side = 8 if peers % 8 == 0 else peers
     other = peers // side
@@ -39,7 +43,7 @@
 
 def kernel(
     tm_size, dm_size, widths_in, x, snr, peaks,
-    widths, widths_sem, ext, low_band, high_band, low_twice, high_twice, box_band, fm, part, det, split, boxed, rows_max,
+    widths, widths_sem, ext, low_band, high_band, low_twice, high_twice, box_band, fm, part, det, split, boxed, acc,
     power_out, power_in, scale, col_out, col_in, common, box_common, peak_out, peak_in,
     edge_sem, load_sem, halo_send, halo_recv, head_send, head_recv,
     power_send, power_recv, col_send, col_recv, peak_send, peak_recv, tm_known, dm_known,
@@ -51,14 +55,14 @@
     total_len = length * tm_size
     tm = lax.axis_index("tm")
     dm = lax.axis_index("dm")
-    right, left = lax.rem(tm + 1, tm_size), lax.rem(tm + tm_size - 1, tm_size)
+    right, left = wrapped(tm + 1, tm_size), wrapped(tm + tm_size - 1, tm_size)
     side, other, steps = peer_offsets(tm_size)
-    tm_x, tm_y = tm // side, tm % side
+    tm_x = tm // side
+    tm_y = tm - tm_x * side
 
     def tm_peer(step):
-        return lax.rem(tm_x + step[0], other) * side + lax.rem(tm_y + step[1], side)
-
-    dm_steps = sorted(range(1, dm_size), key=lambda d: min(d, dm_size - d), reverse=True)
+        return wrapped(tm_x + step[0], other) * side + wrapped(tm_y + step[1], side)
+
 
     spans = [pl.ds(sum(CHUNKS[:q]), CHUNKS[q]) for q in range(len(CHUNKS))]
     edge_loads = []
@@ -73,7 +77,7 @@
             edge_loads[-1].start()
 
     dm_hub = dm_size - 1
-    hub_x, hub_y = other // 2, lax.rem(side // 2 + 1, side)
+    hub_x, hub_y = other // 2, (side // 2 + 1) % side
     tm_hub = hub_x * side + hub_y
     is_first, is_last = tm == 0, tm == tm_size - 1
     near_hub = (tm >= tm_hub - 1) & (tm <= tm_hub + 1)
@@ -201,7 +205,7 @@
     for b in range(1, blocks - 1):
         smooth = (banded(fm[b], low_band[...]) + banded(fm[b + 1], high_band[...])) * inner
         power = power + keep(b, pl.ds(0, rows), ext[b + 1] - smooth)
-    rows_max[0] = power
+    acc[...] = power
 
     for q, span in enumerate(spans):
         @pl.when(jnp.logical_not(is_first))
@@ -218,25 +222,33 @@
         from_after = banded(after, high_twice[...]) * (inner * inner)
         power = keep(0, span, part[0, span] - from_before)
         power = power + keep(blocks - 1, span, part[1, span] - from_after)
-        rows_max[0, span] = rows_max[0, span] + power
+        acc[span, :] = acc[span, :] + power
 
     for h in range(rows // HALF):
-        turned = rows_max[0, pl.ds(h * HALF, HALF)].T
+        turned = acc[pl.ds(h * HALF, HALF), :].T
         power_out[pl.ds(h, 1), :] = jnp.sum(turned, axis=0, keepdims=True)
 
     @pl.when(tm != tm_hub)
     def _():
         pl.semaphore_wait(tm_known, 1)
 
-    def to_peers(src, dst, send_sem, recv_sem):
-        for step in steps:
-            pltpu.make_async_remote_copy(
-                src_ref=src, dst_ref=dst.at[step[0] * side + step[1] - 1],
-                send_sem=send_sem, recv_sem=recv_sem,
-                device_id={"tm": tm_peer(step)}, device_id_type=MESH,
-            ).start()
-
-    to_peers(power_out, power_in, power_send, power_recv)
+    late = lambda d, n: 1.5 * min(d, n - d) + (d > n // 2) + 0.5 * (d == n // 2)
+    reach = lambda p: (p[0] > 0) + 0.1 * min(p[0], other - p[0]) + late(p[1], side)
+    places = sorted(((px, py) for px in range(other) for py in range(side)), key=reach)
+
+    def to_all(src, dst, send_sem, recv_sem, order):
+        for px, py in order:
+            target = px * side + py
+            slot = wrapped(px - tm_x + other, other) * side + wrapped(py - tm_y + side, side) - 1
+
+            @pl.when(tm != target)
+            def _():
+                pltpu.make_async_remote_copy(
+                    src_ref=src, dst_ref=dst.at[slot], send_sem=send_sem, recv_sem=recv_sem,
+                    device_id={"tm": target}, device_id_type=MESH,
+                ).start()
+
+    to_all(power_out, power_in, power_send, power_recv, places[::-1])
     head = pltpu.make_async_remote_copy(
         src_ref=det.at[:, pl.ds(0, HALF)], dst_ref=det.at[:, pl.ds(length, HALF)],
         send_sem=head_send, recv_sem=head_recv,
@@ -290,11 +302,15 @@
             sums[t] = sums[t] + det[pl.ds(r * 8, 8), pl.ds(t * HALF, HALF)] * gain
     for t in range(tiles + 1):
         col_out[pl.ds(t, 1), :] = jnp.sum(sums[t], axis=0, keepdims=True)
-    for d in dm_steps:
-        pltpu.make_async_remote_copy(
-            src_ref=col_out, dst_ref=col_in.at[d - 1], send_sem=col_send, recv_sem=col_recv,
-            device_id={"dm": lax.rem(dm + d, dm_size)}, device_id_type=MESH,
-        ).start()
+    for target in range(dm_size):
+
+        @pl.when(dm != target)
+        def _():
+            pltpu.make_async_remote_copy(
+                src_ref=col_out, dst_ref=col_in.at[wrapped(target - dm + dm_size, dm_size) - 1],
+                send_sem=col_send, recv_sem=col_recv,
+                device_id={"dm": target}, device_id_type=MESH,
+            ).start()
 
     for k, piece in enumerate(parts_of(det[:, pl.ds(length, HALF)])):
         split[k, :, pl.ds(length, HALF)] = piece
@@ -302,8 +318,20 @@
 
     inverse = []
     for i in range(boxes):
-        width = jnp.full((16, HALF), widths[i], jnp.int32).astype(jnp.float32)
+        width = jnp.full((8, HALF), widths[i], jnp.int32).astype(jnp.float32)
         inverse.append(1.0 / jnp.sqrt(width))
+
+    def scale_rows(r, carry):
+        span = pl.ds(pl.multiple_of(r * 8, 8), 8)
+        gain = scale[span, :]
+        for i in range(boxes):
+            gain_i = gain * inverse[i]
+            for t in range(tiles):
+                lanes = pl.ds(i * HALF, HALF)
+                boxed[t, span, lanes] = boxed[t, span, lanes] * gain_i
+        return carry
+
+    lax.fori_loop(0, rows // 8, scale_rows, 0)
 
     pltpu.make_async_copy(col_in, col_in, col_recv).wait()
     column_total = col_out[...] + jnp.sum(col_in[...], axis=0)
@@ -311,32 +339,44 @@
     window = jnp.concatenate([common[pl.ds(0, tiles), :], common[pl.ds(1, tiles), :]], axis=1)
     box_common[...] = banded(window, box_band[pl.ds(0, BLOCK), :])
 
-    for i in range(boxes):
-        offsets = [
-            jnp.broadcast_to(box_common[pl.ds(t, 1), pl.ds(i * HALF, HALF)], (16, HALF)) * inverse[i]
+    halves = rows // HALF
+    offsets = [
+        [
+            jnp.broadcast_to(box_common[pl.ds(t, 1), pl.ds(i * HALF, HALF)], (8, HALF)) * inverse[i]
             for t in range(tiles)
         ]
+        for i in range(boxes)
+    ]
+
+    def series_of(i, t, span):
+        return boxed[t, span, pl.ds(i * HALF, HALF)] - offsets[i][t]
+
+    for i in range(boxes):
+        for h in range(halves):
+            pieces = []
+            for r in range(HALF // 8):
+                span = pl.ds(h * HALF + r * 8, 8)
+                values = [series_of(i, t, span) for t in range(tiles)]
+                while len(values) > 1:
+                    values = [jnp.maximum(a, b) for a, b in zip(values[::2], values[1::2])]
+                pieces.append(values[0])
+            turned = jnp.concatenate(pieces, axis=0).T
+            peak_out[pl.ds(i * halves + h, 1), :] = jnp.max(turned, axis=0, keepdims=True)
+    to_all(peak_out, peak_in, peak_send, peak_recv, places)
+
+    for i in range(boxes):
 
         def some_rows(r, carry):
-            for k in range(4):
-                span = pl.ds(pl.multiple_of(r * 64 + k * 16, 16), 16)
-                gain = scale[span, :] * inverse[i]
-                most = None
-                for t in range(tiles):
-                    series = boxed[t, span, pl.ds(i * HALF, HALF)] * gain - offsets[t]
-                    most = series if most is None else jnp.maximum(most, series)
-                    snr[i, span, pl.ds(t * HALF, HALF)] = series.astype(jnp.bfloat16)
-                rows_max[i, span] = most
+            top = pl.ds(pl.multiple_of(r * 16, 16), 8)
+            bottom = pl.ds(pl.multiple_of(r * 16 + 8, 8), 8)
+            both = pl.ds(pl.multiple_of(r * 16, 16), 16)
+            for t in range(tiles):
+                pair = jnp.concatenate([series_of(i, t, top), series_of(i, t, bottom)], axis=0)
+                snr[i, both, pl.ds(t * HALF, HALF)] = pair.astype(jnp.bfloat16)
             return carry
 
-        lax.fori_loop(0, rows // 64, some_rows, 0)
-
-    halves = rows // HALF
-    for i in range(boxes):
-        for h in range(halves):
-            turned = rows_max[i, pl.ds(h * HALF, HALF)].T
-            peak_out[pl.ds(i * halves + h, 1), :] = jnp.max(turned, axis=0, keepdims=True)
-    to_peers(peak_out, peak_in, peak_send, peak_recv)
+        lax.fori_loop(0, rows // 16, some_rows, 0)
+
     pltpu.make_async_copy(peak_in, peak_in, peak_recv).wait()
     most = jnp.maximum(peak_out[...], jnp.max(peak_in[...], axis=0))
     for i in range(boxes):
@@ -360,10 +400,14 @@
     pltpu.make_async_copy(peak_in, peak_in, peak_send).wait()
 
 
-def hand_out(snr, peaks, snr_out, peaks_out, sems):
-    boxes = snr.shape[0]
-    copies = [pltpu.make_async_copy(peaks, peaks_out, sems.at[boxes])]
-    copies += [pltpu.make_async_copy(snr.at[i], snr_out.at[i], sems.at[i]) for i in range(boxes)]
+def hand_out(snr, peaks, snr_out, peaks_out, peaks_sem, sems):
+    boxes, pieces = sems.shape
+    rows = snr.shape[1] // pieces
+    copies = [pltpu.make_async_copy(peaks, peaks_out, peaks_sem)]
+    for i in range(boxes):
+        for k in range(pieces):
+            span = pl.ds(k * rows, rows)
+            copies.append(pltpu.make_async_copy(snr.at[i, span], snr_out.at[i, span], sems.at[i, k]))
     for copy in copies:
         copy.start()
     for copy in copies:
@@ -402,7 +446,7 @@
                 pltpu.VMEM((rows, length + HALF), f32),
                 pltpu.VMEM((3, rows, length + HALF), bf16),
                 pltpu.VMEM((tiles, rows, boxes * HALF), f32),
-                pltpu.VMEM((boxes, rows, HALF), f32),
+                pltpu.VMEM((rows, HALF), f32),
                 pltpu.VMEM((halves, HALF), f32),
                 pltpu.VMEM((tm_size - 1, halves, HALF), f32),
                 pltpu.VMEM((rows, HALF), f32),
@@ -432,7 +476,7 @@
             ),
             in_specs=[pl.BlockSpec(memory_space=pl.ANY)] * 2,
             out_specs=(pl.BlockSpec(memory_space=pl.ANY),) * 2,
-            scratch_shapes=[dma((boxes + 1,))],
+            scratch_shapes=[dma, dma((boxes, 1))],
             compiler_params=pltpu.CompilerParams(vmem_limit_bytes=2**22),
         )(snr, peaks)
 

time: 41.6 us -> 39.9 us (0.959)
  Pallas kernels: 40.8 us -> 38.7 us
    pallas_call x1, Pallas kernels: 39.4 us -> 37.4 us  [step(): pl.pallas_call(functools.partial(kernel, tm_size, dm_size), out_shape=(pl...]
where the time goes in v4:
time: 39.9 us; the launch traced here: 39.4 us
  Pallas kernels  38.7 us (97%)
  between operations  0.64 us (2%)
    pallas_call x1, Pallas kernels, step(): pl.pallas_call(functools.partial(kernel, tm_size, dm_size), out_shape=(pl...  37.4 us
    pallas_call x1, Pallas kernels, step(): pl.pallas_call(hand_out, out_shape=(jax.ShapeDtypeStruct(snr.shape, bf16)...  1.36 us

profile of v4, /device:TPU:1, one launch (start us, length us, event | category | flops | bytes accessed | tf_op | source)
XLA Modules:
  0.0 39.4 jit_solution(11535662452528719246)
XLA Ops:
  0.6 37.4 %shard_map.41 = (bf16[4,256,1024]{2,1,0:T(8,128)(2,1)S(1)}, f32[4,256]{1,0:T(4,128)S(1)}) custom-call(s32[4]{0:T(128)} %widths_in.1, f32[256,1024]{1,0:T(8,128)} %x.1), custom_call_target="tpu_custom_call" | custom-call | tf_op jit(solution)/shard_map/pallas_call | solution.py:427
  38.0 1.4 %shard_map.42 = (bf16[4,256,1024]{2,1,0:T(8,128)(2,1)}, f32[4,256]{1,0:T(4,128)}) custom-call(bf16[4,256,1024]{2,1,0:T(8,128)(2,1)S(1)} %get-tuple-element.4.snr, f32[4,256]{1,0:T(4,128)S(1)} %get-tuple-element.5.peaks), custom_call_target="tpu_custom_call" | custom-call | tf_op jit(solution)/shard_map/pallas_call | solution.py:471

commit v5 on v4

--- a/solution.py
+++ b/solution.py
@@ -270,11 +270,16 @@
                 jnp.float32
             ).astype(jnp.bfloat16)
 
+    def lanes_of(i, t):
+        return pl.ds((i * tiles + t) * HALF, HALF)
+
     def box_sums(t):
         window = jnp.concatenate(
             [split[k, :, pl.ds(t * HALF, BLOCK)] for k in range(3)], axis=1
         )
-        boxed[t] = jnp.dot(window, box_band[...], preferred_element_type=jnp.float32)
+        sums = jnp.dot(window, box_band[...], preferred_element_type=jnp.float32)
+        for i in range(boxes):
+            boxed[:, lanes_of(i, t)] = sums[:, i * HALF:(i + 1) * HALF]
 
     for t in range(tiles - 1):
         box_sums(t)
@@ -327,8 +332,7 @@
         for i in range(boxes):
             gain_i = gain * inverse[i]
             for t in range(tiles):
-                lanes = pl.ds(i * HALF, HALF)
-                boxed[t, span, lanes] = boxed[t, span, lanes] * gain_i
+                boxed[span, lanes_of(i, t)] = boxed[span, lanes_of(i, t)] * gain_i
         return carry
 
     lax.fori_loop(0, rows // 8, scale_rows, 0)
@@ -349,7 +353,7 @@
     ]
 
     def series_of(i, t, span):
-        return boxed[t, span, pl.ds(i * HALF, HALF)] - offsets[i][t]
+        return boxed[span, lanes_of(i, t)] - offsets[i][t]
 
     for i in range(boxes):
         for h in range(halves):
@@ -445,7 +449,7 @@
                 pltpu.VMEM((2, rows, BLOCK), f32),
                 pltpu.VMEM((rows, length + HALF), f32),
                 pltpu.VMEM((3, rows, length + HALF), bf16),
-                pltpu.VMEM((tiles, rows, boxes * HALF), f32),
+                pltpu.VMEM((rows, boxes * tiles * HALF), f32),
                 pltpu.VMEM((rows, HALF), f32),
                 pltpu.VMEM((halves, HALF), f32),
                 pltpu.VMEM((tm_size - 1, halves, HALF), f32),

time: 39.9 us -> 39.6 us (level)
  no operation moved by 1% of the time
where the time goes in v5:
time: 39.6 us; the launch traced here: 39.1 us
  Pallas kernels  38.5 us (97%)
  between operations  0.64 us (2%)
    pallas_call x1, Pallas kernels, step(): pl.pallas_call(functools.partial(kernel, tm_size, dm_size), out_shape=(pl...  37.1 us
    pallas_call x1, Pallas kernels, step(): pl.pallas_call(hand_out, out_shape=(jax.ShapeDtypeStruct(snr.shape, bf16)...  1.36 us

profile of v5, /device:TPU:1, one launch (start us, length us, event | category | flops | bytes accessed | tf_op | source)
XLA Modules:
  0.0 39.1 jit_solution(17326787313850864972)
XLA Ops:
  0.6 37.1 %shard_map.41 = (bf16[4,256,1024]{2,1,0:T(8,128)(2,1)S(1)}, f32[4,256]{1,0:T(4,128)S(1)}) custom-call(s32[4]{0:T(128)} %widths_in.1, f32[256,1024]{1,0:T(8,128)} %x.1), custom_call_target="tpu_custom_call" | custom-call | tf_op jit(solution)/shard_map/pallas_call | solution.py:431
  37.8 1.4 %shard_map.42 = (bf16[4,256,1024]{2,1,0:T(8,128)(2,1)}, f32[4,256]{1,0:T(4,128)}) custom-call(bf16[4,256,1024]{2,1,0:T(8,128)(2,1)S(1)} %get-tuple-element.4.snr, f32[4,256]{1,0:T(4,128)S(1)} %get-tuple-element.5.peaks), custom_call_target="tpu_custom_call" | custom-call | tf_op jit(solution)/shard_map/pallas_call | solution.py:475

commit v6 on v5

--- a/solution.py
+++ b/solution.py
@@ -11,7 +11,7 @@
 HALF = 128
 BLOCK = 2 * HALF
 EPS = 1e-06
-CHUNKS = (80, 80, 64, 32)
+CHUNKS = (96, 96, 48, 16)
 
 
 def parts_of(x):
@@ -64,6 +64,32 @@
         return wrapped(tm_x + step[0], other) * side + wrapped(tm_y + step[1], side)
 
 
+    dm_hub = dm_size - 1
+    hub_x, hub_y = other // 2, (side // 2 + 1) % side
+    tm_hub = hub_x * side + hub_y
+    is_first, is_last = tm == 0, tm == tm_size - 1
+    near_hub = (tm >= tm_hub - 1) & (tm <= tm_hub + 1)
+    barrier = pltpu.get_barrier_semaphore()
+
+    def greet(peer):
+        pl.semaphore_signal(barrier, inc=1, device_id=peer, device_id_type=MESH)
+
+    @pl.when(jnp.logical_not(is_first))
+    def _():
+        greet({"tm": left})
+
+    @pl.when(jnp.logical_not(is_last))
+    def _():
+        greet({"tm": right})
+
+    @pl.when(jnp.logical_not(near_hub))
+    def _():
+        greet({"tm": tm_hub})
+
+    @pl.when(dm != dm_hub)
+    def _():
+        greet({"dm": dm_hub})
+
     spans = [pl.ds(sum(CHUNKS[:q]), CHUNKS[q]) for q in range(len(CHUNKS))]
     edge_loads = []
     for q, span in enumerate(spans):
@@ -75,32 +101,6 @@
                 )
             )
             edge_loads[-1].start()
-
-    dm_hub = dm_size - 1
-    hub_x, hub_y = other // 2, (side // 2 + 1) % side
-    tm_hub = hub_x * side + hub_y
-    is_first, is_last = tm == 0, tm == tm_size - 1
-    near_hub = (tm >= tm_hub - 1) & (tm <= tm_hub + 1)
-    barrier = pltpu.get_barrier_semaphore()
-
-    def greet(peer):
-        pl.semaphore_signal(barrier, inc=1, device_id=peer, device_id_type=MESH)
-
-    @pl.when(jnp.logical_not(is_first))
-    def _():
-        greet({"tm": left})
-
-    @pl.when(jnp.logical_not(is_last))
-    def _():
-        greet({"tm": right})
-
-    @pl.when(jnp.logical_not(near_hub))
-    def _():
-        greet({"tm": tm_hub})
-
-    @pl.when(dm != dm_hub)
-    def _():
-        greet({"dm": dm_hub})
 
     beside = jnp.minimum(tm, 1) + jnp.minimum(tm_size - 1 - tm, 1)
     greetings = jnp.where(tm == tm_hub, tm_size - 1, beside)
@@ -195,8 +195,6 @@
     part[1] = ext[blocks] - smooth * own_last
 
     def keep(block_idx, span, values):
-        for k, piece in enumerate(parts_of(values)):
-            split[k, span, pl.ds(block_idx * BLOCK, BLOCK)] = piece
         det[span, pl.ds(block_idx * BLOCK, BLOCK)] = values
         squares = values * values
         return squares[:, :HALF] + squares[:, HALF:]
@@ -232,7 +230,7 @@
     def _():
         pl.semaphore_wait(tm_known, 1)
 
-    late = lambda d, n: 1.5 * min(d, n - d) + (d > n // 2) + 0.5 * (d == n // 2)
+    late = lambda d, n: 1.5 * min(d, n - d) + (d > n // 2) + 0.5 * (d == n // 2) - 1.2 * (d == 2)
     reach = lambda p: (p[0] > 0) + 0.1 * min(p[0], other - p[0]) + late(p[1], side)
     places = sorted(((px, py) for px in range(other) for py in range(side)), key=reach)
 
@@ -260,6 +258,10 @@
         head.start()
 
 
+    for b in range(blocks):
+        lanes = pl.ds(b * BLOCK, BLOCK)
+        for k, piece in enumerate(parts_of(det[:, lanes])):
+            split[k, :, lanes] = piece
     fetch.wait()
     lane = lax.broadcasted_iota(jnp.int32, (BLOCK, HALF), 1)
     depth = lax.broadcasted_iota(jnp.int32, (BLOCK, HALF), 0)

time: 39.6 us -> 39.4 us (level)
  no operation moved by 1% of the time
where the time goes in v6:
time: 39.4 us; the launch traced here: 39.1 us
  Pallas kernels  38.5 us (98%)
  between operations  0.64 us (2%)
    pallas_call x1, Pallas kernels, step(): pl.pallas_call(functools.partial(kernel, tm_size, dm_size), out_shape=(pl...  37.1 us
    pallas_call x1, Pallas kernels, step(): pl.pallas_call(hand_out, out_shape=(jax.ShapeDtypeStruct(snr.shape, bf16)...  1.36 us

profile of v6, /device:TPU:1, one launch (start us, length us, event | category | flops | bytes accessed | tf_op | source)
XLA Modules:
  0.0 39.1 jit_solution(13547700911564078786)
XLA Ops:
  0.6 37.1 %shard_map.41 = (bf16[4,256,1024]{2,1,0:T(8,128)(2,1)S(1)}, f32[4,256]{1,0:T(4,128)S(1)}) custom-call(s32[4]{0:T(128)} %widths_in.1, f32[256,1024]{1,0:T(8,128)} %x.1), custom_call_target="tpu_custom_call" | custom-call | tf_op jit(solution)/shard_map/pallas_call | solution.py:433
  37.8 1.4 %shard_map.42 = (bf16[4,256,1024]{2,1,0:T(8,128)(2,1)}, f32[4,256]{1,0:T(4,128)}) custom-call(bf16[4,256,1024]{2,1,0:T(8,128)(2,1)S(1)} %get-tuple-element.4.snr, f32[4,256]{1,0:T(4,128)S(1)} %get-tuple-element.5.peaks), custom_call_target="tpu_custom_call" | custom-call | tf_op jit(solution)/shard_map/pallas_call | solution.py:477

commit v7 on v6

--- a/solution.py
+++ b/solution.py
@@ -214,10 +214,10 @@
         def _():
             to_left[q].wait_recv()
 
-        before = jnp.where(is_first, 0.0, ext[0, span])
-        after = jnp.where(is_last, 0.0, ext[blocks + 1, span])
-        from_before = banded(before, low_twice[...]) * (inner * inner)
-        from_after = banded(after, high_twice[...]) * (inner * inner)
+        before = jnp.where(is_first, 0.0, ext[0, span] * (inner * inner))
+        after = jnp.where(is_last, 0.0, ext[blocks + 1, span] * (inner * inner))
+        from_before = banded(before, low_twice[...])
+        from_after = banded(after, high_twice[...])
         power = keep(0, span, part[0, span] - from_before)
         power = power + keep(blocks - 1, span, part[1, span] - from_after)
         acc[span, :] = acc[span, :] + power

time: 39.4 us -> 39.4 us (level)
  no operation moved by 1% of the time
where the time goes in v7:
time: 39.4 us; the launch traced here: 39.1 us
  Pallas kernels  38.5 us (98%)
  between operations  0.64 us (2%)
    pallas_call x1, Pallas kernels, step(): pl.pallas_call(functools.partial(kernel, tm_size, dm_size), out_shape=(pl...  37.1 us
    pallas_call x1, Pallas kernels, step(): pl.pallas_call(hand_out, out_shape=(jax.ShapeDtypeStruct(snr.shape, bf16)...  1.36 us

profile of v7, /device:TPU:1, one launch (start us, length us, event | category | flops | bytes accessed | tf_op | source)
XLA Modules:
  0.0 39.1 jit_solution(3916729465740867953)
XLA Ops:
  0.6 37.1 %shard_map.41 = (bf16[4,256,1024]{2,1,0:T(8,128)(2,1)S(1)}, f32[4,256]{1,0:T(4,128)S(1)}) custom-call(s32[4]{0:T(128)} %widths_in.1, f32[256,1024]{1,0:T(8,128)} %x.1), custom_call_target="tpu_custom_call" | custom-call | tf_op jit(solution)/shard_map/pallas_call | solution.py:433
  37.8 1.4 %shard_map.42 = (bf16[4,256,1024]{2,1,0:T(8,128)(2,1)}, f32[4,256]{1,0:T(4,128)}) custom-call(bf16[4,256,1024]{2,1,0:T(8,128)(2,1)S(1)} %get-tuple-element.4.snr, f32[4,256]{1,0:T(4,128)S(1)} %get-tuple-element.5.peaks), custom_call_target="tpu_custom_call" | custom-call | tf_op jit(solution)/shard_map/pallas_call | solution.py:477

commit v8 on v7

--- a/solution.py
+++ b/solution.py
@@ -235,16 +235,15 @@
     places = sorted(((px, py) for px in range(other) for py in range(side)), key=reach)
 
     def to_all(src, dst, send_sem, recv_sem, order):
-        for px, py in order:
-            target = px * side + py
-            slot = wrapped(px - tm_x + other, other) * side + wrapped(py - tm_y + side, side) - 1
-
-            @pl.when(tm != target)
-            def _():
-                pltpu.make_async_remote_copy(
-                    src_ref=src, dst_ref=dst.at[slot], send_sem=send_sem, recv_sem=recv_sem,
-                    device_id={"tm": target}, device_id_type=MESH,
-                ).start()
+        names = [px * side + py for px, py in order]
+        rank = sum(jnp.where(tm == name, k, 0) for k, name in enumerate(names))
+        for k in range(tm_size - 1):
+            target = jnp.where(rank <= k, names[k + 1], names[k])
+            pltpu.make_async_remote_copy(
+                src_ref=src, dst_ref=dst.at[tm - jnp.where(tm > target, 1, 0)],
+                send_sem=send_sem, recv_sem=recv_sem,
+                device_id={"tm": target}, device_id_type=MESH,
+            ).start()
 
     to_all(power_out, power_in, power_send, power_recv, places[::-1])
     head = pltpu.make_async_remote_copy(
@@ -309,15 +308,13 @@
             sums[t] = sums[t] + det[pl.ds(r * 8, 8), pl.ds(t * HALF, HALF)] * gain
     for t in range(tiles + 1):
         col_out[pl.ds(t, 1), :] = jnp.sum(sums[t], axis=0, keepdims=True)
-    for target in range(dm_size):
-
-        @pl.when(dm != target)
-        def _():
-            pltpu.make_async_remote_copy(
-                src_ref=col_out, dst_ref=col_in.at[wrapped(target - dm + dm_size, dm_size) - 1],
-                send_sem=col_send, recv_sem=col_recv,
-                device_id={"dm": target}, device_id_type=MESH,
-            ).start()
+    for k in range(dm_size - 1):
+        later = jnp.where(dm <= k, 1, 0)
+        pltpu.make_async_remote_copy(
+            src_ref=col_out, dst_ref=col_in.at[dm - 1 + later],
+            send_sem=col_send, recv_sem=col_recv,
+            device_id={"dm": k + later}, device_id_type=MESH,
+        ).start()
 
     for k, piece in enumerate(parts_of(det[:, pl.ds(length, HALF)])):
         split[k, :, pl.ds(length, HALF)] = piece

time: 39.4 us -> 39.4 us (level)
  no operation moved by 1% of the time
where the time goes in v8:
time: 39.4 us; the launch traced here: 39.2 us
  Pallas kernels  38.5 us (98%)
  between operations  0.64 us (2%)
    pallas_call x1, Pallas kernels, step(): pl.pallas_call(functools.partial(kernel, tm_size, dm_size), out_shape=(pl...  37.2 us
    pallas_call x1, Pallas kernels, step(): pl.pallas_call(hand_out, out_shape=(jax.ShapeDtypeStruct(snr.shape, bf16)...  1.36 us

profile of v8, /device:TPU:1, one launch (start us, length us, event | category | flops | bytes accessed | tf_op | source)
XLA Modules:
  0.0 39.2 jit_solution(3097689060138271975)
XLA Ops:
  0.6 37.2 %shard_map.41 = (bf16[4,256,1024]{2,1,0:T(8,128)(2,1)S(1)}, f32[4,256]{1,0:T(4,128)S(1)}) custom-call(s32[4]{0:T(128)} %widths_in.1, f32[256,1024]{1,0:T(8,128)} %x.1), custom_call_target="tpu_custom_call" | custom-call | tf_op jit(solution)/shard_map/pallas_call | solution.py:430
  37.8 1.4 %shard_map.42 = (bf16[4,256,1024]{2,1,0:T(8,128)(2,1)}, f32[4,256]{1,0:T(4,128)}) custom-call(bf16[4,256,1024]{2,1,0:T(8,128)(2,1)S(1)} %get-tuple-element.4.snr, f32[4,256]{1,0:T(4,128)S(1)} %get-tuple-element.5.peaks), custom_call_target="tpu_custom_call" | custom-call | tf_op jit(solution)/shard_map/pallas_call | solution.py:474
